TPU v7x, 128 devices: a whole 4x4x4 slice. The times are simulated.
128 devices in a mesh: shard: 8 (over x, core), member: 16 (over z, y).
Axes of the slice: x: 4, y: 4, z: 4, core: 2. Of those that a mesh axis runs over, the one named last changes fastest.
Arguments:
- embeddings: float32 [32768, 768], P(('shard', 'member')), may hold values from -1200 to 1200
- clusters: int32 [32768], P(('shard', 'member')), may hold values from 0 to 255, as said below
- row_ids: int32 [32768], P(('shard', 'member')), may hold values from 0 to 32767, each once
- owner_map: int32 [256], replicated, may hold values from 0 to 127, as said below
Outputs:
- centroids: float32 [256, 768], P(('shard', 'member'))
- earlier_max: float32 [32768], P(('shard', 'member'))
Inputs may be any that keep to these rules, and one draw needn't show every extreme that they name: Of the rows of one device, at most 6 lie in clusters of any one owner; one owner index, the same for all devices, gets exactly 6 rows from every device. `owner_map`: every owner index owns exactly 2 clusters.
All inputs are finite; a program needn't handle non-finite values.
Results may differ from a plain program's by a relative error of at most 0.00042.
Values may be sent and summed in bfloat16 or wider, within the bound.
No kernel may reach another device: no remote copies, remote signals or barrier semaphores. Data moves between devices by JAX's collectives and lax.ppermute only.
A program may use at most 64 MiB of HBM per device.

v0:
```python
import math

import jax
import jax.numpy as jnp
from jax import lax
from jax.sharding import PartitionSpec as P

epsilon = 1e-06


def unit_rows(rows):
    return (rows * lax.rsqrt(jnp.sum(rows * rows, axis=1, keepdims=True) + epsilon)).astype(
        jnp.bfloat16
    )


def lookup(entries, values_table):
    matches = entries[:, None] == jnp.arange(values_table.shape[0], dtype=jnp.int32)[None, :]
    found = jnp.sum(jnp.where(matches, values_table[None, :], 0), axis=1)
    return (found, jnp.any(matches, axis=1))


def earlier_side(queries, query_ids, query_groups, key_unit, key_ids, key_groups):
    scores = lax.dot_general(
        queries, key_unit, (((1,), (1,)), ((), ())), preferred_element_type=jnp.float32
    )
    allowed = (query_groups[:, None] == key_groups[None, :]) & (
        key_ids[None, :] < query_ids[:, None]
    )
    return jnp.max(jnp.where(allowed, scores, -1.0), axis=1)


def shards(embeddings, clusters, row_ids, owner_map):
    owners = lax.axis_size("shard") * lax.axis_size("member")
    local_rows = embeddings.shape[0]
    feature_width = embeddings.shape[1]
    cluster_count = owner_map.shape[0]
    per_owner = cluster_count // owners
    capacity = 3 * local_rows // owners
    slots = owners * capacity
    positions = jnp.arange(cluster_count, dtype=jnp.int32)
    same_owner = owner_map[None, :] == owner_map[:, None]
    owner_rank = jnp.sum(
        (same_owner & (positions[None, :] < positions[:, None])).astype(jnp.int32), axis=1
    )
    owner_of, _ = lookup(clusters, owner_map)
    matches = owner_of[:, None] == jnp.arange(owners, dtype=jnp.int32)[None, :]
    running = jnp.cumsum(matches.astype(jnp.int32), axis=0)
    slot_index = jnp.sum(jnp.where(matches, running - 1, 0), axis=1)
    send_index = owner_of * capacity + slot_index
    slot_ids = jnp.full((slots,), -1, jnp.int32).at[send_index].set(row_ids)
    slot_groups = jnp.full((slots,), -1, jnp.int32).at[send_index].set(clusters)
    packed = jnp.zeros((slots, feature_width), jnp.float32).at[send_index].set(embeddings)
    received, recv_ids, groups = (
        lax.all_to_all(packed, ("shard", "member"), split_axis=0, concat_axis=0, tiled=True),
        lax.all_to_all(slot_ids, ("shard", "member"), split_axis=0, concat_axis=0, tiled=True),
        lax.all_to_all(slot_groups, ("shard", "member"), split_axis=0, concat_axis=0, tiled=True),
    )
    normed = unit_rows(received)
    local_rank, present = lookup(groups, owner_rank)
    selector = (
        (local_rank[None, :] == jnp.arange(per_owner, dtype=jnp.int32)[:, None]) & present[None, :]
    ).astype(jnp.float32)
    owner_total = jnp.dot(
        selector, received, precision=lax.Precision.HIGHEST, preferred_element_type=jnp.float32
    )
    block_rows = math.gcd(slots, 512)
    block_count = slots // block_rows

    def block_max(inputs):
        query_block, query_groups, query_ids = inputs
        return earlier_side(query_block, query_ids, query_groups, normed, recv_ids, groups)

    running_max = lax.map(
        block_max,
        (
            normed.reshape(block_count, block_rows, feature_width),
            groups.reshape(block_count, block_rows),
            recv_ids.reshape(block_count, block_rows),
        ),
    ).reshape(slots)
    returned = lax.all_to_all(
        running_max, ("shard", "member"), split_axis=0, concat_axis=0, tiled=True
    )
    earlier_max = returned[send_index]
    centroids = owner_total * lax.rsqrt(
        jnp.mean(owner_total * owner_total, axis=1, keepdims=True) + epsilon
    )
    return (centroids, earlier_max)


def solution(mesh):
    placed = (P(("shard", "member"), None), P(("shard", "member")), P(("shard", "member")), P())
    return jax.shard_map(
        shards,
        mesh=mesh,
        in_specs=placed,
        out_specs=(P(("shard", "member"), None), P(("shard", "member"))),
        check_vma=False,
    )
```

profile of v0, /device:TPU:1, one launch (start us, length us, event | category | flops | bytes accessed | tf_op | source)
XLA Modules:
  0.0 115.9 jit_solution(6086304606892789844)
XLA Ops:
  0.6 1.0 convert_reduce_fusion
  2.3 1.6 %scatter_custom_fusion = s32[768]{0:T(1024)S(1)} fusion(s32[256]{0:T(256)S(1)} %bitcast.46, s32[256]{0:T(256)} %param.7, s32[]{:T(128)} %constant.18.clone.1), kind=kCustom, calls=%fused_computation.45 | custom fusion | bytes 3584 | tf_op jit(solution)/shard_map/scatter | solution.py:52
  3.9 0.8 all_to_all.32
  4.6 11.5 %all-to-all-start = ((s32[128,6,1]{1,2,0:T(1,128)}), s32[128,6,1]{1,2,0:T(1,128)S(1)}, u32[]{:S(2)}, u32[]{:S(2)}) async-start(s32[128,6,1]{1,2,0:T(1,128)} %bitcast.10), calls=%async_computation | async-start | bytes 131072 | tf_op jit(solution)/shard_map/all_to_all | solution.py:57
  16.1 1.6 %scatter_custom_fusion.2 = s32[768]{0:T(1024)S(1)} fusion(s32[256]{0:T(256)S(1)} %bitcast.47, s32[256]{0:T(256)} %param.8, s32[]{:T(128)} %constant.18.clone.1), kind=kCustom, calls=%fused_computation.43 | custom fusion | bytes 3584 | tf_op jit(solution)/shard_map/scatter | solution.py:51
  17.7 0.8 all_to_all.37
  18.4 7.5 %all-to-all-done = s32[128,6,1]{1,2,0:T(1,128)S(1)} async-done(((s32[128,6,1]{1,2,0:T(1,128)}), s32[128,6,1]{1,2,0:T(1,128)S(1)}, u32[]{:S(2)}, u32[]{:S(2)}) %all-to-all-start) | async-done | bytes 3104 | tf_op jit(solution)/shard_map/all_to_all | solution.py:57
  25.9 4.3 %all-to-all-start.2 = ((s32[128,6,1]{1,2,0:T(1,128)}), s32[128,6,1]{1,2,0:T(1,128)S(1)}, u32[]{:S(2)}, u32[]{:S(2)}) async-start(s32[128,6,1]{1,2,0:T(1,128)} %bitcast.11), calls=%async_computation.2 | async-start | bytes 131072 | tf_op jit(solution)/shard_map/all_to_all | solution.py:56
  30.2 2.6 %scatter_custom_fusion.1 = f32[768,768]{1,0:T(8,128)S(1)} fusion(s32[256]{0:T(256)S(1)} %bitcast.48, f32[256,768]{1,0:T(8,128)} %param.6, f32[]{:T(128)} %constant.11.clone.1), kind=kCustom, calls=%fused_computation.14 | custom fusion | bytes 2359808 | tf_op jit(solution)/shard_map/scatter | solution.py:53
  32.8 1.8 %all_to_all.34 = f32[128,6,768]{2,1,0:T(8,128)} reshape(f32[768,768]{1,0:T(8,128)S(1)} %scatter_custom_fusion.1) | data formatting | bytes 4718592 | tf_op jit(solution)/shard_map/all_to_all | solution.py:55
  34.6 5.4 %all-to-all-done.2 = s32[128,6,1]{1,2,0:T(1,128)S(1)} async-done(((s32[128,6,1]{1,2,0:T(1,128)}), s32[128,6,1]{1,2,0:T(1,128)S(1)}, u32[]{:S(2)}, u32[]{:S(2)}) %all-to-all-start.2) | async-done | bytes 3104 | tf_op jit(solution)/shard_map/all_to_all | solution.py:56
  40.0 4.4 %all-to-all-start.1 = ((f32[128,6,768]{2,1,0:T(8,128)}), f32[128,6,768]{2,1,0:T(8,128)S(1)}, u32[]{:S(2)}, u32[]{:S(2)}) async-start(f32[128,6,768]{2,1,0:T(8,128)} %all_to_all.34), calls=%async_computation.1 | async-start | bytes 6291456 | tf_op jit(solution)/shard_map/all_to_all | solution.py:55
  44.7 0.5 broadcast.122
  45.2 0.8 reduce.15
  46.2 0.8 reduce.14
  47.8 36.9 %all-to-all-done.1 = f32[128,6,768]{2,1,0:T(8,128)S(1)} async-done(((f32[128,6,768]{2,1,0:T(8,128)}), f32[128,6,768]{2,1,0:T(8,128)S(1)}, u32[]{:S(2)}, u32[]{:S(2)}) %all-to-all-start.1) | async-done | bytes 2359328 | tf_op jit(solution)/shard_map/all_to_all | solution.py:55
  85.3 1.6 %all_to_all.36 = f32[768,768]{1,0:T(8,128)} reshape(f32[128,6,768]{2,1,0:T(8,128)S(1)} %all-to-all-done.1) | data formatting | bytes 4718592 | tf_op jit(solution)/shard_map/all_to_all | solution.py:55
  86.9 3.0 %multiply_convert_fusion = bf16[768,768]{1,0:T(8,128)(2,1)} fusion(f32[768,768]{1,0:T(8,128)} %all_to_all.36, f32[768]{0:T(1024)S(1)} %rsqrt.26), kind=kLoop, calls=%fused_computation.12 | loop fusion | flops 1179648 | bytes 3542016 | tf_op jit(solution)/shard_map/convert_element_type | solution.py:12
  89.9 1.0 multiply_reduce_fusion.1
  91.0 1.6 %all_to_all.40 = f32[3,256,768]{2,1,0:T(8,128)} reshape(f32[128,6,768]{2,1,0:T(8,128)S(1)} %all-to-all-done.1) | data formatting | bytes 4718592 | tf_op jit(solution)/shard_map/all_to_all | solution.py:55
  92.6 1.9 %multiply_convert_fusion.1 = bf16[3,256,768]{2,1,0:T(8,128)(2,1)S(1)} fusion(f32[3,256,768]{2,1,0:T(8,128)} %all_to_all.40, f32[3,256]{1,0:T(4,128)S(1)} %rsqrt.25), kind=kLoop, calls=%fused_computation.13 | loop fusion | flops 1179648 | bytes 3542016 | tf_op jit(solution)/shard_map/convert_element_type | solution.py:12
  94.5 2.0 %while.10 = (s32[]{:T(128)}, f32[3,256]{1,0:T(4,128)S(1)}, s32[3,256]{1,0:T(4,128)S(1)}, s32[768]{0:T(1024)S(1)}, s32[768]{0:T(1024)S(1)}, /*index=5*/s32[3,256]...) while((s32[]{:T(128)}, f32[3,256]{1,0:T(4,128)S(1)}, ...), condition=%wide.region_14.15_spmd, body=%wide.region_12.14_spmd.sunk | while | flops 302972672 | bytes 1590393 | solution.py:74
  94.6 0.6 fusion.29
  95.2 0.6 fusion.29
  95.9 0.6 fusion.29
  96.6 0.8 all_to_all.41
  97.3 5.3 %all-to-all-start.3 = ((f32[128,6,1]{1,2,0:T(1,128)}), f32[128,6,1]{1,2,0:T(1,128)S(1)}, u32[]{:S(2)}, u32[]{:S(2)}) async-start(f32[128,6,1]{1,2,0:T(1,128)} %bitcast.12), calls=%async_computation.3 | async-start | bytes 131072 | tf_op jit(solution)/shard_map/all_to_all | solution.py:82
  102.7 0.7 broadcast_multiply_fusion
  103.4 9.1 %all-to-all-done.3 = f32[128,6,1]{1,2,0:T(1,128)S(1)} async-done(((f32[128,6,1]{1,2,0:T(1,128)}), f32[128,6,1]{1,2,0:T(1,128)S(1)}, u32[]{:S(2)}, u32[]{:S(2)}) %all-to-all-start.3) | async-done | bytes 3104 | tf_op jit(solution)/shard_map/all_to_all | solution.py:82
  112.5 0.5 broadcast.124
  113.0 0.8 reduce.16
  114.0 1.9 %gather_fusion = f32[256]{0:T(256)} fusion(f32[768]{0:T(1024)S(1)} %all_to_all.43, s32[1024]{0:T(1024)S(1)} %pad_clamp_fusion), kind=kCustom, calls=%fused_computation | custom fusion | bytes 3072 | tf_op jit(solution)/shard_map/gather | solution.py:85
  (34 shorter events, 2.8 us)
Async XLA Ops:
  4.6 21.3 %all-to-all-start = ((s32[128,6,1]{1,2,0:T(1,128)}), s32[128,6,1]{1,2,0:T(1,128)S(1)}, u32[]{:S(2)}, u32[]{:S(2)}) async-start(s32[128,6,1]{1,2,0:T(1,128)} %bitcast.10), calls=%async_computation | async-start | bytes 131072 | tf_op jit(solution)/shard_map/all_to_all | solution.py:57
  25.9 14.1 %all-to-all-start.2 = ((s32[128,6,1]{1,2,0:T(1,128)}), s32[128,6,1]{1,2,0:T(1,128)S(1)}, u32[]{:S(2)}, u32[]{:S(2)}) async-start(s32[128,6,1]{1,2,0:T(1,128)} %bitcast.11), calls=%async_computation.2 | async-start | bytes 131072 | tf_op jit(solution)/shard_map/all_to_all | solution.py:56
  40.0 44.6 %all-to-all-start.1 = ((f32[128,6,768]{2,1,0:T(8,128)}), f32[128,6,768]{2,1,0:T(8,128)S(1)}, u32[]{:S(2)}, u32[]{:S(2)}) async-start(f32[128,6,768]{2,1,0:T(8,128)} %all_to_all.34), calls=%async_computation.1 | async-start | bytes 6291456 | tf_op jit(solution)/shard_map/all_to_all | solution.py:55
  86.9 3.0 %copy-start = (f32[768,768]{1,0:T(8,128)S(1)}, f32[768,768]{1,0:T(8,128)}, u32[]{:S(2)}) copy-start(f32[768,768]{1,0:T(8,128)} %all_to_all.36) | copy-start | bytes 7077892
  92.6 2.0 %copy-start.1 = (bf16[768,768]{1,0:T(8,128)(2,1)S(1)}, bf16[768,768]{1,0:T(8,128)(2,1)}, u32[]{:S(2)}) copy-start(bf16[768,768]{1,0:T(8,128)(2,1)} %multiply_convert_fusion) | copy-start | bytes 3538948
  97.3 15.2 %all-to-all-start.3 = ((f32[128,6,1]{1,2,0:T(1,128)}), f32[128,6,1]{1,2,0:T(1,128)S(1)}, u32[]{:S(2)}, u32[]{:S(2)}) async-start(f32[128,6,1]{1,2,0:T(1,128)} %bitcast.12), calls=%async_computation.3 | async-start | bytes 131072 | tf_op jit(solution)/shard_map/all_to_all | solution.py:82
where the time goes:
time: 116 us
  waiting for transfers between devices  58.9 us (51%)
  starting transfers between devices  25.5 us (22%)
  local copies, waits for them, and re-layouts  17.2 us (15%)
  other arithmetic  10.6 us (9%)
  matrix products  2.83 us (2%)
    all_to_all x1, waiting for transfers between devices, shards(): lax.all_to_all(packed, ('shard', 'member'), split_axis=0, concat_axis=0,...  36.9 us
    all_to_all x1, starting transfers between devices, shards(): lax.all_to_all(slot_groups, ('shard', 'member'), split_axis=0, concat_axi...  11.5 us
    all_to_all x1, waiting for transfers between devices, shards(): lax.all_to_all(running_max, ('shard', 'member'), split_axis=0, concat_axi...  9.14 us
    all_to_all x1, waiting for transfers between devices, shards(): lax.all_to_all(slot_groups, ('shard', 'member'), split_axis=0, concat_axi...  7.49 us
    all_to_all x1, waiting for transfers between devices, shards(): lax.all_to_all(slot_ids, ('shard', 'member'), split_axis=0, concat_axis=0...  5.35 us
    all_to_all x1, starting transfers between devices, shards(): lax.all_to_all(running_max, ('shard', 'member'), split_axis=0, concat_axi...  5.35 us
    all_to_all x3, local copies, waits for them, and re-layouts, shards(): lax.all_to_all(packed, ('shard', 'member'), split_axis=0, concat_axis=0,...  5.05 us
    convert_element_type x2, other arithmetic, unit_rows(): (rows * lax.rsqrt(jnp.sum(rows * rows, axis=1, keepdims=True) + epsilon))...  4.97 us
  transfers between devices with their start and end apart: 4, of which 4 were waited for; matrix products, arithmetic and copies ran while one was open for 7% of the time, Pallas kernels for 0%

commit v1 on v0

v1 whole, which is shorter than its diff:
```python
import jax
import jax.numpy as jnp
from jax import lax
from jax.experimental import pallas as pl
from jax.experimental.pallas import tpu as pltpu
from jax.sharding import PartitionSpec as P

epsilon = 1e-06
axes = ("shard", "member")
sent_rows = 8
lanes = 128
id_base = 256
id_range = 32768
f32 = jnp.float32
bf16 = jnp.bfloat16
i32 = jnp.int32


def iota(shape, dim):
    return lax.broadcasted_iota(i32, shape, dim)


def dot(a, b, contract=((1,), (0,))):
    return lax.dot_general(a, b, (contract, ((), ())), preferred_element_type=f32)


def one_hot(mask):
    return jnp.where(mask, 1.0, 0.0).astype(bf16)


def column(row):
    n = row.shape[1]
    diagonal = iota((n, n), 0) == iota((n, n), 1)
    spread = jnp.where(diagonal, row.astype(f32), 0.0).astype(bf16)
    return dot(spread, jnp.ones((n, n), bf16))


def earlier_equal(row):
    n = row.shape[1]
    before = iota((n, n), 0) < iota((n, n), 1)
    hits = before & (column(row) == row.astype(f32))
    return jnp.sum(jnp.where(hits, 1.0, 0.0), axis=0, keepdims=True)


def pack_kernel(rows_ref, clusters_ref, ids_ref, owners_ref, sent_ref, route_ref):
    rows = rows_ref[...]
    clusters = clusters_ref[...]
    ids = ids_ref[...]
    owner_map = owners_ref[...]
    row_count, width = rows.shape
    slot_count = sent_ref.shape[0]
    cluster_count = owner_map.shape[1]

    rank_map = earlier_equal(owner_map)
    sub = iota((8, cluster_count), 0)
    table = jnp.where(sub == 0, owner_map.astype(f32), jnp.where(sub == 1, rank_map, 0.0))
    cluster_hot = one_hot(iota((cluster_count, row_count), 0) == clusters)
    found = dot(table.astype(bf16), cluster_hot)
    owner = found[0:1].astype(i32)
    rank = found[1:2].astype(i32)
    slot = earlier_equal(owner).astype(i32)
    target = owner * sent_rows + slot
    spill = owner * sent_rows + (sent_rows - 2) + rank

    power = jnp.sum(rows * rows, axis=1, keepdims=True) + epsilon
    inverse = lax.rsqrt(power)
    unit = (rows * inverse).astype(bf16)
    norm = (power * inverse).astype(bf16)
    residual = (rows - unit.astype(f32) * norm.astype(f32)).astype(bf16)

    high = ids // id_base
    sub = iota((lanes, row_count), 0)
    notes = jnp.where(sub == 0, high, 0)
    notes = jnp.where(sub == 1, ids - high * id_base, notes)
    notes = jnp.where(sub == 2, rank + 1, notes).astype(f32).astype(bf16)
    norm_lane = jnp.where(iota((row_count, lanes), 1) == 3, norm.astype(f32), 0.0).astype(bf16)

    place = iota((slot_count, row_count), 0)
    take = one_hot(place == target)
    take_spill = one_hot(place == spill)
    sent_ref[:, :width] = (dot(take, unit) + dot(take_spill, residual)).astype(bf16)
    sent_ref[:, width:] = (dot(take, notes, ((1,), (1,))) + dot(take, norm_lane)).astype(bf16)
    sub = iota(route_ref.shape, 0)
    route_ref[...] = jnp.where(sub == 0, owner, slot)


def score_kernel(got_ref, sums_ref, best_ref, *, block):
    slot_count = got_ref.shape[0]
    width = got_ref.shape[1] - lanes
    notes = got_ref[:, width:]

    sub = iota((8, lanes), 0)
    lane = iota((8, lanes), 1)
    pick = jnp.where((sub == 0) & (lane == 0), float(id_base), 0.0)
    pick = jnp.where((sub == 0) & (lane == 1), 1.0, pick)
    pick = jnp.where((sub == 0) & (lane == 2), float(id_range), pick)
    pick = jnp.where((sub == 1) & (lane == 2), 1.0, pick)
    pick = jnp.where((sub == 2) & (lane == 3), 1.0, pick).astype(bf16)
    wide = dot(pick, notes, ((1,), (1,)))
    key_row = wide[0:1]
    rank_row = wide[1:2]
    norm_row = wide[2:3]
    base_row = rank_row * float(id_range)
    lane = iota((lanes, lanes), 0)
    spread = jnp.where(lane == 0, float(id_base), 0.0)
    spread = jnp.where(lane == 1, 1.0, spread)
    spread = jnp.where(lane == 2, float(id_range), spread).astype(bf16)
    key_col = dot(notes, spread)

    sub = iota((8, slot_count), 0)
    within = iota((8, slot_count), 1) % sent_rows
    weight = jnp.where(rank_row == (sub + 1).astype(f32), norm_row, 0.0)
    weight = weight + jnp.where(within == sub + (sent_rows - 2), 1.0, 0.0)
    sums = dot(weight.astype(bf16), got_ref[:, :width])
    sums = sums[0 : sums_ref.shape[0]]
    scale = lax.rsqrt(jnp.mean(sums * sums, axis=1, keepdims=True) + epsilon)
    sums_ref[...] = sums * scale

    keys = got_ref[:, :width]
    for start in range(0, slot_count, block):
        stop = start + block
        scores = dot(keys, got_ref[start:stop, :width], ((1,), (1,)))
        low = base_row[:, start:stop]
        high = key_row[:, start:stop]
        other = jnp.concatenate([key_col] * (block // lanes), axis=1)
        allowed = (other >= low) & (other < high)
        best = jnp.max(jnp.where(allowed, scores, -1.0), axis=0, keepdims=True)
        peers = block // sent_rows
        mine = iota((peers, block), 1) // sent_rows == iota((peers, block), 0)
        spread_best = jnp.where(mine, best, 0.0)
        lane_of = one_hot(iota((block, lanes), 0) % sent_rows == iota((block, lanes), 1))
        best_ref[start // sent_rows : stop // sent_rows, :] = exact_dot(spread_best, lane_of)


def exact_dot(values, hot, contract=((1,), (0,))):
    first = values.astype(bf16)
    rest = values - first.astype(f32)
    second = rest.astype(bf16)
    third = (rest - second.astype(f32)).astype(bf16)
    return dot(first, hot, contract) + dot(second, hot, contract) + dot(third, hot, contract)


def unpack_kernel(back_ref, route_ref, out_ref):
    owner = route_ref[0:1, :]
    slot = route_ref[1:2, :]
    back = back_ref[...]
    row_count = owner.shape[1]
    hot = one_hot(iota((back.shape[0], row_count), 0) == owner)
    found = exact_dot(back, hot, ((0,), (0,)))[0:8]
    mine = iota((8, row_count), 0) == slot
    out_ref[...] = jnp.sum(jnp.where(mine, found, 0.0), axis=0, keepdims=True)


def shards(embeddings, clusters, row_ids, owner_map):
    owners = lax.axis_size("shard") * lax.axis_size("member")
    local_rows, width = embeddings.shape
    cluster_count = owner_map.shape[0]
    per_owner = cluster_count // owners
    slots = owners * sent_rows
    packed, route = pl.pallas_call(
        pack_kernel,
        out_shape=(
            jax.ShapeDtypeStruct((slots, width + lanes), bf16),
            jax.ShapeDtypeStruct((8, local_rows), i32),
        ),
        name="pack",
    )(
        embeddings,
        clusters.reshape(1, local_rows),
        row_ids.reshape(1, local_rows),
        owner_map.reshape(1, cluster_count),
    )
    received = lax.all_to_all(packed, axes, split_axis=0, concat_axis=0, tiled=True)
    centroids, best = pl.pallas_call(
        lambda *refs: score_kernel(*refs, block=256),
        out_shape=(
            jax.ShapeDtypeStruct((per_owner, width), f32),
            jax.ShapeDtypeStruct((owners, lanes), f32),
        ),
        name="score",
    )(received)
    returned = lax.all_to_all(
        best.reshape(owners, 1, lanes), axes, split_axis=0, concat_axis=0, tiled=True
    )
    earlier_max = pl.pallas_call(
        unpack_kernel,
        out_shape=jax.ShapeDtypeStruct((1, local_rows), f32),
        name="unpack",
    )(returned.reshape(owners, lanes), route)
    return (centroids, earlier_max.reshape(local_rows))


def solution(mesh):
    placed = (P(axes, None), P(axes), P(axes), P())
    return jax.shard_map(
        shards,
        mesh=mesh,
        in_specs=placed,
        out_specs=(P(axes, None), P(axes)),
        check_vma=False,
    )
```

time: 116 us -> 67.4 us (0.58)
  waiting for transfers between devices: 58.9 us -> 0 us
  blocking collectives: 0 us -> 54.3 us
  starting transfers between devices: 25.5 us -> 0 us
  local copies, waits for them, and re-layouts: 17.2 us -> 0 us
  Pallas kernels: 0 us -> 12.2 us
  other arithmetic: 10.6 us -> 0 us
  matrix products: 2.83 us -> 0 us
    all_to_all x4 -> x0, waiting for transfers between devices: 58.9 us -> none  [the longest x1 36.9 us: shards(): lax.all_to_all(packed, ('shard', 'member'), split_axis=0, concat_axis=0,...]
    all_to_all x0 -> x2, blocking collectives: none -> 54.3 us  [the longest x1 38.3 us: shards(): lax.all_to_all(packed, axes, split_axis=0, concat_axis=0, tiled=True)]
    all_to_all x4 -> x0, starting transfers between devices: 25.5 us -> none  [the longest x1 11.5 us: shards(): lax.all_to_all(slot_groups, ('shard', 'member'), split_axis=0, concat_axi...]
    pallas_call x0 -> x3, Pallas kernels: none -> 12.2 us  [the longest x1 6.49 us: shards(): pl.pallas_call(lambda *refs: score_kernel(*refs, block=256), out_shape=(j...]
    all_to_all x10 -> x0, local copies, waits for them, and re-layouts: 8.6 us -> none  [the longest x3 5.05 us: shards(): lax.all_to_all(packed, ('shard', 'member'), split_axis=0, concat_axis=0,...]
    scatter x3 -> x0, local copies, waits for them, and re-layouts: 5.71 us -> none  [the longest x1 2.59 us: shards(): jnp.zeros((slots, feature_width), jnp.float32).at[send_index]]
    convert_element_type x2 -> x0, other arithmetic: 4.97 us -> none  [unit_rows(): (rows * lax.rsqrt(jnp.sum(rows * rows, axis=1, keepdims=True) + epsilon))...]
    dot_general x4 -> x0, matrix products: 2.83 us -> none  [the longest x3 1.83 us: earlier_side(): lax.dot_general(queries, key_unit, (((1,), (1,)), ((), ())), preferred_el...]
  transfers between devices with their start and end apart: 4 -> 0, of which waited for: 4 -> 0; matrix products, arithmetic and copies ran while one was open for 7% -> 0% of each run, Pallas kernels for 0% -> 0%
where the time goes in v1:
time: 67.4 us; the launch traced here: 67.1 us
  blocking collectives  54.3 us (81%)
  Pallas kernels  12.2 us (18%)
    all_to_all x1, blocking collectives, shards(): lax.all_to_all(packed, axes, split_axis=0, concat_axis=0, tiled=True)  38.3 us
    all_to_all x1, blocking collectives, shards(): lax.all_to_all(best.reshape(owners, 1, lanes), axes, split_axis=0, concat...  16 us
    pallas_call x1, Pallas kernels, shards(): pl.pallas_call(lambda *refs: score_kernel(*refs, block=256), out_shape=(j...  6.49 us
    pallas_call x1, Pallas kernels, shards(): pl.pallas_call(pack_kernel, out_shape=(jax.ShapeDtypeStruct((slots, width...  4.07 us
    pallas_call x1, Pallas kernels, shards(): pl.pallas_call(unpack_kernel, out_shape=jax.ShapeDtypeStruct((1, local_ro...  1.62 us

profile of v1, /device:TPU:1, one launch (start us, length us, event | category | flops | bytes accessed | tf_op | source)
XLA Modules:
  0.0 67.1 jit_solution(10592230527889493637)
XLA Ops:
  0.6 4.1 %pack.1 = (bf16[1024,896]{1,0:T(8,128)(2,1)}, s32[8,256]{1,0:T(8,128)}) custom-call(f32[256,768]{1,0:T(8,128)} %rows_ref.1, s32[1,256]{1,0:T(1,128)} %bitcast.14, s32[1,256]{1,0:T(1,128)} %bitcast.15, s32[1,256]{1,0:T(1,128)} %bitcast.16), custom_call_target="tpu_custom_call" | custom-call | tf_op jit(solution)/shard_map/pack/pallas_call | solution.py:160
  4.7 38.3 %all_to_all.16 = bf16[128,8,896]{2,1,0:T(8,128)(2,1)} all-to-all(bf16[128,8,896]{2,1,0:T(8,128)(2,1)} %bitcast.11), channel_id=1, replica_groups=mesh['shard'=8,'member'=16] {'shard','member'}, dimensions={0} | all-to-all | bytes 3670016 | tf_op jit(solution)/shard_map/all_to_all | solution.py:173
  43.0 6.5 %score.1 = (f32[2,768]{1,0:T(2,128)}, f32[128,128]{1,0:T(8,128)}) custom-call(bf16[1024,896]{1,0:T(8,128)(2,1)} %bitcast.10), custom_call_target="tpu_custom_call" | custom-call | tf_op jit(solution)/shard_map/score/pallas_call | solution.py:174
  49.4 16.0 %all_to_all.17 = f32[128,1,128]{2,1,0:T(1,128)} all-to-all(f32[128,1,128]{2,1,0:T(1,128)} %bitcast.13), channel_id=1, replica_groups=mesh['shard'=8,'member'=16] {'shard','member'}, dimensions={0} | all-to-all | bytes 131072 | tf_op jit(solution)/shard_map/all_to_all | solution.py:182
  65.5 1.6 %unpack.1 = f32[1,256]{1,0:T(1,128)} custom-call(f32[128,128]{1,0:T(8,128)} %bitcast.12, s32[8,256]{1,0:T(8,128)} %get-tuple-element.9.route_ref), custom_call_target="tpu_custom_call" | custom-call | tf_op jit(solution)/shard_map/unpack/pallas_call | solution.py:185

commit v2 on v1

v2 whole, which is shorter than its diff:
```python
import jax
import jax.numpy as jnp
from jax import lax
from jax.experimental import pallas as pl
from jax.experimental.pallas import tpu as pltpu
from jax.sharding import PartitionSpec as P

epsilon = 1e-06
axes = ("shard", "member")
pairs = 3
lanes = 128
id_base = 256
id_range = 32768
f32 = jnp.float32
bf16 = jnp.bfloat16
i32 = jnp.int32
params = pltpu.CompilerParams(vmem_limit_bytes=24 << 20)


def iota(shape, dim):
    return lax.broadcasted_iota(i32, shape, dim)


def dot(a, b, contract=((1,), (0,))):
    return lax.dot_general(a, b, (contract, ((), ())), preferred_element_type=f32)


def one_hot(mask):
    return jnp.where(mask, 1.0, 0.0).astype(bf16)


def count(mask):
    return jnp.sum(jnp.where(mask, 1.0, 0.0), axis=0, keepdims=True)


def pack_kernel(
    rows_hbm,
    clusters_hbm,
    ids_hbm,
    owners_hbm,
    sent_ref,
    route_ref,
    rows_ref,
    clusters_ref,
    ids_ref,
    owners_ref,
    sems,
):
    index_copies = (
        pltpu.make_async_copy(owners_hbm, owners_ref, sems.at[0]),
        pltpu.make_async_copy(clusters_hbm, clusters_ref, sems.at[1]),
        pltpu.make_async_copy(ids_hbm, ids_ref, sems.at[2]),
    )
    copy = pltpu.make_async_copy(rows_hbm, rows_ref, sems.at[3])
    for index_copy in index_copies:
        index_copy.start()
    copy.start()
    for index_copy in index_copies:
        index_copy.wait()
    clusters = clusters_ref[...]
    ids = ids_ref[...]
    owner_map = owners_ref[...].astype(f32)
    row_count, width = rows_ref.shape
    owners = sent_ref.shape[0]
    cluster_count = owner_map.shape[1]

    square = (cluster_count, cluster_count)
    diagonal = iota(square, 0) == iota(square, 1)
    before = iota(square, 0) < iota(square, 1)
    spread = jnp.where(diagonal, owner_map, 0.0).astype(bf16)
    map_col = dot(spread, jnp.ones(square, bf16))
    rank_map = count(before & (map_col == owner_map))
    sub = iota((8, cluster_count), 0)
    table = jnp.where(sub == 0, owner_map, jnp.where(sub == 1, rank_map, 0.0)).astype(bf16)
    cluster_hot = one_hot(iota((cluster_count, row_count), 0) == clusters)
    found = dot(table, cluster_hot)
    owner_col = dot(cluster_hot, map_col[:, :row_count].astype(bf16), ((0,), (0,)))
    slot = count(before & (owner_col == found[0:1])).astype(i32)
    owner = found[0:1].astype(i32)
    rank = found[1:2].astype(i32)
    pair = slot // 2
    target = owner * 2 + slot % 2

    copy.wait()
    rows = rows_ref[...]
    power = jnp.sum(rows * rows, axis=1, keepdims=True) + epsilon
    inverse = lax.rsqrt(power)
    unit = (rows * inverse).astype(bf16)
    norm = (power * inverse).astype(bf16).astype(f32)
    residual = (rows - unit.astype(f32) * norm).astype(bf16)
    norm_row = jnp.sum(jnp.where(diagonal, norm, 0.0), axis=0, keepdims=True)

    high = ids // id_base
    lane = iota((lanes, row_count), 0)
    field = jnp.where(lane // 4 == pair, lane % 4, -1)
    notes = jnp.where(field == 0, high.astype(f32), 0.0)
    notes = jnp.where(field == 1, (ids - high * id_base).astype(f32), notes)
    notes = jnp.where(field == 2, (rank + 1).astype(f32), notes)
    notes = jnp.where(field == 3, norm_row, notes).astype(bf16)

    place = iota((2 * owners, row_count), 0)
    for p in range(pairs):
        take = one_hot(place == jnp.where(pair == p, target, -1))
        part = dot(take, unit).astype(bf16).reshape(owners, 2, width)
        sent_ref[:, :, p * width : (p + 1) * width] = part
    take = one_hot(place == owner * 2 + rank)
    part = dot(take, residual).astype(bf16).reshape(owners, 2, width)
    sent_ref[:, :, pairs * width : (pairs + 1) * width] = part
    take = one_hot(place == target)
    part = dot(take, notes, ((1,), (1,))).astype(bf16).reshape(owners, 2, lanes)
    sent_ref[:, :, (pairs + 1) * width :] = part
    sub = iota(route_ref.shape, 0)
    route_ref[...] = jnp.where(sub == 0, target, pair)


def score_kernel(got_ref, sums_ref, best_ref):
    owners = got_ref.shape[0]
    width = (got_ref.shape[2] - lanes) // (pairs + 1)
    block = 2 * owners
    notes = got_ref[:, :, (pairs + 1) * width :].reshape(block, lanes)
    keys = []
    for p in range(pairs):
        keys.append(got_ref[:, :, p * width : (p + 1) * width].reshape(block, width))
    residual = got_ref[:, :, pairs * width : (pairs + 1) * width].reshape(block, width)

    sub = iota((8 * pairs, lanes), 0)
    field = iota((8 * pairs, lanes), 1) - 4 * (sub // 8)
    kind = sub % 8
    pick = jnp.where((kind == 0) & (field == 0), float(id_base), 0.0)
    pick = jnp.where((kind == 0) & (field == 1), 1.0, pick)
    pick = jnp.where((kind == 0) & (field == 2), float(id_range), pick)
    pick = jnp.where((kind == 1) & (field == 2), 1.0, pick)
    pick = jnp.where((kind == 2) & (field == 3), 1.0, pick).astype(bf16)
    wide = dot(pick, notes, ((1,), (1,)))
    field = iota((lanes, pairs * lanes), 0) - 4 * (iota((lanes, pairs * lanes), 1) // lanes)
    spread = jnp.where(field == 0, float(id_base), 0.0)
    spread = jnp.where(field == 1, 1.0, spread)
    spread = jnp.where(field == 2, float(id_range), spread).astype(bf16)
    key_col = dot(notes, spread)

    sub = iota((8, block), 0)
    sums = dot(one_hot(iota((8, block), 1) % 2 == sub), residual)
    for p in range(pairs):
        ranks = wide[8 * p + 1 : 8 * p + 2]
        norms = wide[8 * p + 2 : 8 * p + 3]
        weight = jnp.where(ranks == (sub + 1).astype(f32), norms, 0.0)
        sums = sums + dot(weight.astype(bf16), keys[p])
    sums = sums[0 : sums_ref.shape[0]]
    scale = lax.rsqrt(jnp.mean(sums * sums, axis=1, keepdims=True) + epsilon)
    sums_ref[...] = sums * scale

    bests = jnp.full((lanes, block), -1.0, f32)
    for q in range(pairs):
        high = wide[8 * q : 8 * q + 1]
        low = wide[8 * q + 1 : 8 * q + 2] * float(id_range)
        best = jnp.full((1, block), -1.0, f32)
        for p in range(pairs):
            scores = dot(keys[p], keys[q], ((1,), (1,)))
            other = key_col[:, p * lanes : (p + 1) * lanes]
            other = jnp.concatenate([other] * (block // lanes), axis=1)
            allowed = (other >= low) & (other < high)
            found = jnp.max(jnp.where(allowed, scores, -1.0), axis=0, keepdims=True)
            best = jnp.maximum(best, found)
        bests = jnp.where(iota((lanes, block), 0) == q, best, bests)
    best_ref[...] = bests.T


def exact_dot(values, hot, contract=((1,), (0,))):
    first = values.astype(bf16)
    rest = values - first.astype(f32)
    second = rest.astype(bf16)
    third = (rest - second.astype(f32)).astype(bf16)
    return dot(first, hot, contract) + dot(second, hot, contract) + dot(third, hot, contract)


def unpack_kernel(back_ref, route_ref, out_ref):
    target = route_ref[0:1, :]
    pair = route_ref[1:2, :]
    back = back_ref[...]
    row_count = target.shape[1]
    hot = one_hot(iota((back.shape[0], row_count), 0) == target)
    found = exact_dot(back, hot, ((0,), (0,)))[0:8]
    mine = iota((8, row_count), 0) == pair
    out_ref[...] = jnp.sum(jnp.where(mine, found, 0.0), axis=0, keepdims=True)


def shards(embeddings, clusters, row_ids, owner_map):
    owners = lax.axis_size("shard") * lax.axis_size("member")
    local_rows, width = embeddings.shape
    cluster_count = owner_map.shape[0]
    per_owner = cluster_count // owners
    hbm = pl.BlockSpec(memory_space=pltpu.HBM)
    packed, route = pl.pallas_call(
        pack_kernel,
        in_specs=[hbm] * 4,
        out_shape=(
            jax.ShapeDtypeStruct((owners, 2, (pairs + 1) * width + lanes), bf16),
            jax.ShapeDtypeStruct((8, local_rows), i32),
        ),
        scratch_shapes=[
            pltpu.VMEM((local_rows, width), f32),
            pltpu.VMEM((1, local_rows), i32),
            pltpu.VMEM((1, local_rows), i32),
            pltpu.VMEM((1, cluster_count), i32),
            pltpu.SemaphoreType.DMA((4,)),
        ],
        compiler_params=params,
        name="pack",
    )(
        *[
            pltpu.with_memory_space_constraint(x, pltpu.HBM)
            for x in (
                embeddings,
                clusters.reshape(1, local_rows),
                row_ids.reshape(1, local_rows),
                owner_map.reshape(1, cluster_count),
            )
        ]
    )
    received = lax.all_to_all(packed, axes, split_axis=0, concat_axis=0, tiled=True)
    centroids, best = pl.pallas_call(
        score_kernel,
        out_shape=(
            jax.ShapeDtypeStruct((per_owner, width), f32),
            jax.ShapeDtypeStruct((2 * owners, lanes), f32),
        ),
        compiler_params=params,
        name="score",
    )(received)
    returned = lax.all_to_all(
        best.reshape(owners, 2, lanes), axes, split_axis=0, concat_axis=0, tiled=True
    )
    earlier_max = pl.pallas_call(
        unpack_kernel,
        out_shape=jax.ShapeDtypeStruct((1, local_rows), f32),
        compiler_params=params,
        name="unpack",
    )(returned.reshape(2 * owners, lanes), route)
    return (centroids, earlier_max.reshape(local_rows))


def solution(mesh):
    placed = (P(axes, None), P(axes), P(axes), P())
    return jax.shard_map(
        shards,
        mesh=mesh,
        in_specs=placed,
        out_specs=(P(axes, None), P(axes)),
        check_vma=False,
    )
```

time: 67.4 us -> 56.2 us (0.83)
  Pallas kernels: 12.2 us -> 4.53 us
  blocking collectives: 54.3 us -> 50.8 us
    pallas_call x2, Pallas kernels: 10.6 us -> 3.71 us  [the longest x1 2.06 us: shards(): pl.pallas_call(pack_kernel, in_specs=[hbm] * 4, out_shape=(jax.ShapeDtype...]
    all_to_all x1, blocking collectives: 38.3 us -> 35.9 us  [shards(): lax.all_to_all(packed, axes, split_axis=0, concat_axis=0, tiled=True)]
    all_to_all x1, blocking collectives: 16 us -> 14.9 us  [shards(): lax.all_to_all(best.reshape(owners, 2, lanes), axes, split_axis=0, concat...]
    pallas_call x1, Pallas kernels: 1.62 us -> 0.81 us  [shards(): pl.pallas_call(unpack_kernel, out_shape=jax.ShapeDtypeStruct((1, local_ro...]
where the time goes in v2:
time: 56.2 us; the launch traced here: 56 us
  blocking collectives  50.8 us (90%)
  Pallas kernels  4.53 us (8%)
  between operations  0.65 us (1%)
    all_to_all x1, blocking collectives, shards(): lax.all_to_all(packed, axes, split_axis=0, concat_axis=0, tiled=True)  35.9 us
    all_to_all x1, blocking collectives, shards(): lax.all_to_all(best.reshape(owners, 2, lanes), axes, split_axis=0, concat...  14.9 us
    pallas_call x1, Pallas kernels, shards(): pl.pallas_call(pack_kernel, in_specs=[hbm] * 4, out_shape=(jax.ShapeDtype...  2.06 us
    pallas_call x1, Pallas kernels, shards(): pl.pallas_call(score_kernel, out_shape=(jax.ShapeDtypeStruct((per_owner,...  1.65 us

profile of v2, /device:TPU:1, one launch (start us, length us, event | category | flops | bytes accessed | tf_op | source)
XLA Modules:
  0.0 56.0 jit_solution(13285152649418895876)
XLA Ops:
  0.6 2.1 %pack.1 = (bf16[128,2,3200]{2,1,0:T(2,128)(2,1)S(1)}, s32[8,256]{1,0:T(8,128)S(1)}) custom-call(f32[256,768]{1,0:T(8,128)} %rows_hbm.1, s32[1,256]{1,0:T(1,128)} %bitcast.8, s32[1,256]{1,0:T(1,128)} %bitcast.9, s32[1,256]{1,0:T(1,128)} %bitcast.10), custom_call_target="tpu_custom_call" | custom-call | tf_op jit(solution)/shard_map/pack/pallas_call | solution.py:193
  2.7 35.9 %all_to_all.10.got_ref = bf16[128,2,3200]{2,1,0:T(2,128)(2,1)S(1)} all-to-all(bf16[128,2,3200]{2,1,0:T(2,128)(2,1)S(1)} %get-tuple-element.6), channel_id=1, replica_groups=mesh['shard'=8,'member'=16] {'shard','member'}, dimensions={0} | all-to-all | bytes 3276800 | tf_op jit(solution)/shard_map/all_to_all | solution.py:220
  38.6 1.7 %score.1 = (f32[2,768]{1,0:T(2,128)}, f32[256,128]{1,0:T(8,128)S(1)}) custom-call(bf16[128,2,3200]{2,1,0:T(2,128)(2,1)S(1)} %all_to_all.10.got_ref), custom_call_target="tpu_custom_call" | custom-call | tf_op jit(solution)/shard_map/score/pallas_call | solution.py:221
  40.3 14.9 %all_to_all.11 = f32[128,2,128]{2,1,0:T(2,128)S(1)} all-to-all(f32[128,2,128]{2,1,0:T(2,128)S(1)} %bitcast.7), channel_id=1, replica_groups=mesh['shard'=8,'member'=16] {'shard','member'}, dimensions={0} | all-to-all | bytes 262144 | tf_op jit(solution)/shard_map/all_to_all | solution.py:230
  55.2 0.8 %unpack.1 = f32[1,256]{1,0:T(1,128)} custom-call(f32[256,128]{1,0:T(8,128)S(1)} %bitcast.6, s32[8,256]{1,0:T(8,128)S(1)} %get-tuple-element.9.route_ref), custom_call_target="tpu_custom_call" | custom-call | tf_op jit(solution)/shard_map/unpack/pallas_call | solution.py:233

commit v3 on v2

--- a/solution.py
+++ b/solution.py
@@ -11,9 +11,14 @@
 lanes = 128
 id_base = 256
 id_range = 32768
+full = 32767.0
+fields = 16
+norm_unit = 256
+norm_bytes = 6
 f32 = jnp.float32
 bf16 = jnp.bfloat16
 i32 = jnp.int32
+i16 = jnp.int16
 params = pltpu.CompilerParams(vmem_limit_bytes=24 << 20)
 
 
@@ -31,6 +36,16 @@
 
 def count(mask):
     return jnp.sum(jnp.where(mask, 1.0, 0.0), axis=0, keepdims=True)
+
+
+def to_bytes(values, unit, n):
+    digits = []
+    rest = values * (1.0 / unit)
+    for _ in range(n):
+        digit = jnp.floor(rest)
+        digits.append(digit)
+        rest = (rest - digit) * id_base
+    return digits
 
 
 def pack_kernel(
@@ -85,67 +100,89 @@
     rows = rows_ref[...]
     power = jnp.sum(rows * rows, axis=1, keepdims=True) + epsilon
     inverse = lax.rsqrt(power)
-    unit = (rows * inverse).astype(bf16)
-    norm = (power * inverse).astype(bf16).astype(f32)
-    residual = (rows - unit.astype(f32) * norm).astype(bf16)
+    norm = power * inverse
+    largest = jnp.max(jnp.abs(rows), axis=1, keepdims=True) * inverse
+    step = jnp.clip(jnp.ceil(largest * full), 1.0, full)
+    codes = jnp.floor(rows * (inverse * (full * full / step)) + 0.5)
+    codes = jnp.clip(codes, -full, full)
+    upper = jnp.floor(codes * (1.0 / id_base)) * id_base
+    halves = jnp.concatenate([upper.astype(bf16), (codes - upper).astype(bf16)], axis=0)
     norm_row = jnp.sum(jnp.where(diagonal, norm, 0.0), axis=0, keepdims=True)
-
-    high = ids // id_base
+    step_row = jnp.sum(jnp.where(diagonal, step, 0.0), axis=0, keepdims=True)
+
+    values = to_bytes(ids.astype(f32), id_base, 2)
+    values = values + [(rank + 1).astype(f32)]
+    values = values + to_bytes(step_row, id_base, 2)
+    values = values + to_bytes(norm_row, norm_unit, norm_bytes)
     lane = iota((lanes, row_count), 0)
-    field = jnp.where(lane // 4 == pair, lane % 4, -1)
-    notes = jnp.where(field == 0, high.astype(f32), 0.0)
-    notes = jnp.where(field == 1, (ids - high * id_base).astype(f32), notes)
-    notes = jnp.where(field == 2, (rank + 1).astype(f32), notes)
-    notes = jnp.where(field == 3, norm_row, notes).astype(bf16)
+    field = jnp.where(lane // fields == pair, lane % fields, -1)
+    notes = jnp.zeros((lanes, row_count), f32)
+    for k, value in enumerate(values):
+        notes = jnp.where(field == k, value, notes)
+    notes = notes.astype(bf16)
 
     place = iota((2 * owners, row_count), 0)
     for p in range(pairs):
         take = one_hot(place == jnp.where(pair == p, target, -1))
-        part = dot(take, unit).astype(bf16).reshape(owners, 2, width)
+        part = dot(jnp.concatenate([take, take], axis=1), halves)
+        part = part.astype(i32).astype(i16).reshape(owners, 2, width)
         sent_ref[:, :, p * width : (p + 1) * width] = part
-    take = one_hot(place == owner * 2 + rank)
-    part = dot(take, residual).astype(bf16).reshape(owners, 2, width)
-    sent_ref[:, :, pairs * width : (pairs + 1) * width] = part
     take = one_hot(place == target)
-    part = dot(take, notes, ((1,), (1,))).astype(bf16).reshape(owners, 2, lanes)
-    sent_ref[:, :, (pairs + 1) * width :] = part
+    part = dot(take, notes, ((1,), (1,)))
+    part = part.astype(i32).astype(i16).reshape(owners, 2, lanes)
+    sent_ref[:, :, pairs * width :] = part
     sub = iota(route_ref.shape, 0)
     route_ref[...] = jnp.where(sub == 0, target, pair)
 
 
 def score_kernel(got_ref, sums_ref, best_ref):
     owners = got_ref.shape[0]
-    width = (got_ref.shape[2] - lanes) // (pairs + 1)
+    width = (got_ref.shape[2] - lanes) // pairs
     block = 2 * owners
-    notes = got_ref[:, :, (pairs + 1) * width :].reshape(block, lanes)
-    keys = []
-    for p in range(pairs):
-        keys.append(got_ref[:, :, p * width : (p + 1) * width].reshape(block, width))
-    residual = got_ref[:, :, pairs * width : (pairs + 1) * width].reshape(block, width)
+    notes = got_ref[:, :, pairs * width :].reshape(block, lanes)
+    notes = notes.astype(i32).astype(f32).astype(bf16)
 
     sub = iota((8 * pairs, lanes), 0)
-    field = iota((8 * pairs, lanes), 1) - 4 * (sub // 8)
+    field = iota((8 * pairs, lanes), 1) - fields * (sub // 8)
     kind = sub % 8
     pick = jnp.where((kind == 0) & (field == 0), float(id_base), 0.0)
     pick = jnp.where((kind == 0) & (field == 1), 1.0, pick)
     pick = jnp.where((kind == 0) & (field == 2), float(id_range), pick)
     pick = jnp.where((kind == 1) & (field == 2), 1.0, pick)
-    pick = jnp.where((kind == 2) & (field == 3), 1.0, pick).astype(bf16)
-    wide = dot(pick, notes, ((1,), (1,)))
-    field = iota((lanes, pairs * lanes), 0) - 4 * (iota((lanes, pairs * lanes), 1) // lanes)
-    spread = jnp.where(field == 0, float(id_base), 0.0)
-    spread = jnp.where(field == 1, 1.0, spread)
-    spread = jnp.where(field == 2, float(id_range), spread).astype(bf16)
-    key_col = dot(notes, spread)
+    for k in range(norm_bytes):
+        weight = float(norm_unit) / float(id_base) ** k
+        pick = jnp.where((kind == 2) & (field == 5 + k), weight, pick)
+    wide = dot(pick.astype(bf16), notes, ((1,), (1,)))
+    shape = (lanes, 2 * pairs * lanes)
+    column = iota(shape, 1) // lanes
+    field = iota(shape, 0) - fields * (column % pairs)
+    keyed = column < pairs
+    spread = jnp.where(field == jnp.where(keyed, 0, 3), float(id_base), 0.0)
+    spread = jnp.where(field == jnp.where(keyed, 1, 4), 1.0, spread)
+    spread = jnp.where(keyed & (field == 2), float(id_range), spread).astype(bf16)
+    tall = dot(notes, spread)
+    key_col = tall[:, : pairs * lanes]
 
     sub = iota((8, block), 0)
-    sums = dot(one_hot(iota((8, block), 1) % 2 == sub), residual)
+    keys = []
+    sums = jnp.zeros((8, width), f32)
     for p in range(pairs):
+        codes = got_ref[:, :, p * width : (p + 1) * width].reshape(block, width)
+        step = tall[:, (pairs + p) * lanes : (pairs + p + 1) * lanes] * (1.0 / (full * full))
+        step = jnp.concatenate([step] * (width // lanes), axis=1)
+        exact = codes.astype(i32).astype(f32) * step
+        unit = exact.astype(bf16)
+        rest = (exact - unit.astype(f32)).astype(bf16)
+        keys.append(unit)
         ranks = wide[8 * p + 1 : 8 * p + 2]
         norms = wide[8 * p + 2 : 8 * p + 3]
-        weight = jnp.where(ranks == (sub + 1).astype(f32), norms, 0.0)
-        sums = sums + dot(weight.astype(bf16), keys[p])
-    sums = sums[0 : sums_ref.shape[0]]
+        coarse = norms.astype(bf16).astype(f32)
+        weight = jnp.where(sub < 2, coarse, norms - coarse)
+        weight = jnp.where(ranks == (sub % 2 + 1).astype(f32), weight, 0.0)
+        weight = jnp.where(sub < 4, weight, 0.0).astype(bf16)
+        sums = sums + dot(weight, unit) + dot(weight, rest)
+    owned = sums_ref.shape[0]
+    sums = sums[0:owned] + sums[owned : 2 * owned]
     scale = lax.rsqrt(jnp.mean(sums * sums, axis=1, keepdims=True) + epsilon)
     sums_ref[...] = sums * scale
 
@@ -194,7 +231,7 @@
         pack_kernel,
         in_specs=[hbm] * 4,
         out_shape=(
-            jax.ShapeDtypeStruct((owners, 2, (pairs + 1) * width + lanes), bf16),
+            jax.ShapeDtypeStruct((owners, 2, pairs * width + lanes), i16),
             jax.ShapeDtypeStruct((8, local_rows), i32),
         ),
         scratch_shapes=[

time: 56.2 us -> 53.9 us (0.959)
  blocking collectives: 50.8 us -> 46.7 us
  Pallas kernels: 4.53 us -> 6.33 us
    all_to_all x1, blocking collectives: 35.9 us -> 32.1 us  [shards(): lax.all_to_all(packed, axes, split_axis=0, concat_axis=0, tiled=True)]
    pallas_call x1, Pallas kernels: 1.65 us -> 3.07 us  [shards(): pl.pallas_call(score_kernel, out_shape=(jax.ShapeDtypeStruct((per_owner,...]
where the time goes in v3:
time: 53.9 us; the launch traced here: 53.7 us
  blocking collectives  46.7 us (87%)
  Pallas kernels  6.33 us (12%)
  between operations  0.64 us (1%)
    all_to_all x1, blocking collectives, shards(): lax.all_to_all(packed, axes, split_axis=0, concat_axis=0, tiled=True)  32.1 us
    all_to_all x1, blocking collectives, shards(): lax.all_to_all(best.reshape(owners, 2, lanes), axes, split_axis=0, concat...  14.6 us
    pallas_call x1, Pallas kernels, shards(): pl.pallas_call(score_kernel, out_shape=(jax.ShapeDtypeStruct((per_owner,...  3.07 us
    pallas_call x1, Pallas kernels, shards(): pl.pallas_call(pack_kernel, in_specs=[hbm] * 4, out_shape=(jax.ShapeDtype...  2.44 us

profile of v3, /device:TPU:1, one launch (start us, length us, event | category | flops | bytes accessed | tf_op | source)
XLA Modules:
  0.0 53.7 jit_solution(14310100812079974109)
XLA Ops:
  0.6 2.4 %pack.1 = (s16[128,2,2432]{2,1,0:T(2,128)(2,1)S(1)}, s32[8,256]{1,0:T(8,128)S(1)}) custom-call(f32[256,768]{1,0:T(8,128)} %rows_hbm.1, s32[1,256]{1,0:T(1,128)} %bitcast.8, s32[1,256]{1,0:T(1,128)} %bitcast.9, s32[1,256]{1,0:T(1,128)} %bitcast.10), custom_call_target="tpu_custom_call" | custom-call | tf_op jit(solution)/shard_map/pack/pallas_call | solution.py:230
  3.1 32.1 %all_to_all.10.got_ref = s16[128,2,2432]{2,1,0:T(2,128)(2,1)S(1)} all-to-all(s16[128,2,2432]{2,1,0:T(2,128)(2,1)S(1)} %get-tuple-element.6), channel_id=1, replica_groups=mesh['shard'=8,'member'=16] {'shard','member'}, dimensions={0} | all-to-all | bytes 2490368 | tf_op jit(solution)/shard_map/all_to_all | solution.py:257
  35.2 3.1 %score.1 = (f32[2,768]{1,0:T(2,128)}, f32[256,128]{1,0:T(8,128)S(1)}) custom-call(s16[128,2,2432]{2,1,0:T(2,128)(2,1)S(1)} %all_to_all.10.got_ref), custom_call_target="tpu_custom_call" | custom-call | tf_op jit(solution)/shard_map/score/pallas_call | solution.py:258
  38.2 14.6 %all_to_all.11 = f32[128,2,128]{2,1,0:T(2,128)S(1)} all-to-all(f32[128,2,128]{2,1,0:T(2,128)S(1)} %bitcast.7), channel_id=1, replica_groups=mesh['shard'=8,'member'=16] {'shard','member'}, dimensions={0} | all-to-all | bytes 262144 | tf_op jit(solution)/shard_map/all_to_all | solution.py:267
  52.9 0.8 %unpack.1 = f32[1,256]{1,0:T(1,128)} custom-call(f32[256,128]{1,0:T(8,128)S(1)} %bitcast.6, s32[8,256]{1,0:T(8,128)S(1)} %get-tuple-element.9.route_ref), custom_call_target="tpu_custom_call" | custom-call | tf_op jit(solution)/shard_map/unpack/pallas_call | solution.py:270

commit v4 on v3

--- a/solution.py
+++ b/solution.py
@@ -135,13 +135,34 @@
     route_ref[...] = jnp.where(sub == 0, target, pair)
 
 
-def score_kernel(got_ref, sums_ref, best_ref):
+def read_notes(got_ref):
+    owners = got_ref.shape[0]
+    notes = got_ref[:, :, got_ref.shape[2] - lanes :].reshape(2 * owners, lanes)
+    return notes.astype(i32).astype(f32).astype(bf16)
+
+
+def read_rows(got_ref, p, step):
     owners = got_ref.shape[0]
     width = (got_ref.shape[2] - lanes) // pairs
-    block = 2 * owners
-    notes = got_ref[:, :, pairs * width :].reshape(block, lanes)
-    notes = notes.astype(i32).astype(f32).astype(bf16)
-
+    codes = got_ref[:, :, p * width : (p + 1) * width].reshape(2 * owners, width)
+    step = jnp.concatenate([step * (1.0 / (full * full))] * (width // lanes), axis=1)
+    return codes.astype(i32).astype(f32) * step
+
+
+def along_sublanes(notes, first, third):
+    shape = (lanes, pairs * lanes)
+    field = iota(shape, 0) - fields * (iota(shape, 1) // lanes)
+    spread = jnp.where(field == first, float(id_base), 0.0)
+    spread = jnp.where(field == first + 1, 1.0, spread)
+    if third is not None:
+        spread = jnp.where(field == third, float(id_range), spread)
+    tall = dot(notes, spread.astype(bf16))
+    return [tall[:, p * lanes : (p + 1) * lanes] for p in range(pairs)]
+
+
+def score_kernel(got_ref, best_ref):
+    block = 2 * got_ref.shape[0]
+    notes = read_notes(got_ref)
     sub = iota((8 * pairs, lanes), 0)
     field = iota((8 * pairs, lanes), 1) - fields * (sub // 8)
     kind = sub % 8
@@ -149,42 +170,10 @@
     pick = jnp.where((kind == 0) & (field == 1), 1.0, pick)
     pick = jnp.where((kind == 0) & (field == 2), float(id_range), pick)
     pick = jnp.where((kind == 1) & (field == 2), 1.0, pick)
-    for k in range(norm_bytes):
-        weight = float(norm_unit) / float(id_base) ** k
-        pick = jnp.where((kind == 2) & (field == 5 + k), weight, pick)
     wide = dot(pick.astype(bf16), notes, ((1,), (1,)))
-    shape = (lanes, 2 * pairs * lanes)
-    column = iota(shape, 1) // lanes
-    field = iota(shape, 0) - fields * (column % pairs)
-    keyed = column < pairs
-    spread = jnp.where(field == jnp.where(keyed, 0, 3), float(id_base), 0.0)
-    spread = jnp.where(field == jnp.where(keyed, 1, 4), 1.0, spread)
-    spread = jnp.where(keyed & (field == 2), float(id_range), spread).astype(bf16)
-    tall = dot(notes, spread)
-    key_col = tall[:, : pairs * lanes]
-
-    sub = iota((8, block), 0)
-    keys = []
-    sums = jnp.zeros((8, width), f32)
-    for p in range(pairs):
-        codes = got_ref[:, :, p * width : (p + 1) * width].reshape(block, width)
-        step = tall[:, (pairs + p) * lanes : (pairs + p + 1) * lanes] * (1.0 / (full * full))
-        step = jnp.concatenate([step] * (width // lanes), axis=1)
-        exact = codes.astype(i32).astype(f32) * step
-        unit = exact.astype(bf16)
-        rest = (exact - unit.astype(f32)).astype(bf16)
-        keys.append(unit)
-        ranks = wide[8 * p + 1 : 8 * p + 2]
-        norms = wide[8 * p + 2 : 8 * p + 3]
-        coarse = norms.astype(bf16).astype(f32)
-        weight = jnp.where(sub < 2, coarse, norms - coarse)
-        weight = jnp.where(ranks == (sub % 2 + 1).astype(f32), weight, 0.0)
-        weight = jnp.where(sub < 4, weight, 0.0).astype(bf16)
-        sums = sums + dot(weight, unit) + dot(weight, rest)
-    owned = sums_ref.shape[0]
-    sums = sums[0:owned] + sums[owned : 2 * owned]
-    scale = lax.rsqrt(jnp.mean(sums * sums, axis=1, keepdims=True) + epsilon)
-    sums_ref[...] = sums * scale
+    key = along_sublanes(notes, 0, 2)
+    step = along_sublanes(notes, 3, None)
+    keys = [read_rows(got_ref, p, step[p]).astype(bf16) for p in range(pairs)]
 
     bests = jnp.full((lanes, block), -1.0, f32)
     for q in range(pairs):
@@ -193,13 +182,44 @@
         best = jnp.full((1, block), -1.0, f32)
         for p in range(pairs):
             scores = dot(keys[p], keys[q], ((1,), (1,)))
-            other = key_col[:, p * lanes : (p + 1) * lanes]
-            other = jnp.concatenate([other] * (block // lanes), axis=1)
+            other = jnp.concatenate([key[p]] * (block // lanes), axis=1)
             allowed = (other >= low) & (other < high)
             found = jnp.max(jnp.where(allowed, scores, -1.0), axis=0, keepdims=True)
             best = jnp.maximum(best, found)
         bests = jnp.where(iota((lanes, block), 0) == q, best, bests)
     best_ref[...] = bests.T
+
+
+def centre_kernel(got_ref, sums_ref):
+    owned, width = sums_ref.shape
+    block = 2 * got_ref.shape[0]
+    notes = read_notes(got_ref)
+    sub = iota((8 * pairs, lanes), 0)
+    field = iota((8 * pairs, lanes), 1) - fields * (sub // 8)
+    kind = sub % 8
+    pick = jnp.where((kind == 1) & (field == 2), 1.0, 0.0)
+    for k in range(norm_bytes):
+        weight = float(norm_unit) / float(id_base) ** k
+        pick = jnp.where((kind == 0) & (field == 5 + k), weight, pick)
+    wide = dot(pick.astype(bf16), notes, ((1,), (1,)))
+    step = along_sublanes(notes, 3, None)
+
+    sub = iota((8, block), 0)
+    sums = jnp.zeros((8, width), f32)
+    for p in range(pairs):
+        exact = read_rows(got_ref, p, step[p])
+        unit = exact.astype(bf16)
+        rest = (exact - unit.astype(f32)).astype(bf16)
+        norms = wide[8 * p : 8 * p + 1]
+        ranks = wide[8 * p + 1 : 8 * p + 2]
+        coarse = norms.astype(bf16).astype(f32)
+        weight = jnp.where(sub < owned, coarse, norms - coarse)
+        weight = jnp.where(ranks == (sub % owned + 1).astype(f32), weight, 0.0)
+        weight = jnp.where(sub < 2 * owned, weight, 0.0).astype(bf16)
+        sums = sums + dot(weight, unit) + dot(weight, rest)
+    sums = sums[0:owned] + sums[owned : 2 * owned]
+    scale = lax.rsqrt(jnp.mean(sums * sums, axis=1, keepdims=True) + epsilon)
+    sums_ref[...] = sums * scale
 
 
 def exact_dot(values, hot, contract=((1,), (0,))):
@@ -255,14 +275,20 @@
         ]
     )
     received = lax.all_to_all(packed, axes, split_axis=0, concat_axis=0, tiled=True)
-    centroids, best = pl.pallas_call(
+    best = pl.pallas_call(
         score_kernel,
-        out_shape=(
-            jax.ShapeDtypeStruct((per_owner, width), f32),
-            jax.ShapeDtypeStruct((2 * owners, lanes), f32),
+        out_shape=jax.ShapeDtypeStruct((2 * owners, lanes), f32),
+        compiler_params=params,
+        name="score",
+    )(received)
+    centroids = pl.pallas_call(
+        centre_kernel,
+        out_shape=jax.ShapeDtypeStruct((per_owner, width), f32),
+        cost_estimate=pl.CostEstimate(
+            flops=200_000_000, bytes_accessed=1_300_000, transcendentals=0
         ),
         compiler_params=params,
-        name="score",
+        name="centre",
     )(received)
     returned = lax.all_to_all(
         best.reshape(owners, 2, lanes), axes, split_axis=0, concat_axis=0, tiled=True

time: 53.9 us -> 53.8 us (level)
  blocking collectives: 46.7 us -> 32.1 us
  waiting for transfers between devices: 0 us -> 7.96 us
  starting transfers between devices: 0 us -> 4.75 us
  Pallas kernels: 6.33 us -> 8.23 us
    all_to_all x1 -> x0, blocking collectives: 14.6 us -> none  [shards(): lax.all_to_all(best.reshape(owners, 2, lanes), axes, split_axis=0, concat...]
    all_to_all x0 -> x1, waiting for transfers between devices: none -> 7.96 us  [shards(): lax.all_to_all(best.reshape(owners, 2, lanes), axes, split_axis=0, concat...]
    all_to_all x0 -> x1, starting transfers between devices: none -> 4.75 us  [shards(): lax.all_to_all(best.reshape(owners, 2, lanes), axes, split_axis=0, concat...]
    pallas_call x1 -> x2, Pallas kernels: 3.07 us -> 4.98 us  [the longest x1 2.6 us: shards(): pl.pallas_call(score_kernel, out_shape=jax.ShapeDtypeStruct((2 * owners,...]
  transfers between devices with their start and end apart: 0 -> 1, of which waited for: 0 -> 1; matrix products, arithmetic and copies ran while one was open for 0% -> 0% of each run, Pallas kernels for 0% -> 4%
where the time goes in v4:
time: 53.8 us; the launch traced here: 53.7 us
  blocking collectives  32.1 us (60%)
  Pallas kernels  8.23 us (15%)
  waiting for transfers between devices  7.96 us (15%)
  starting transfers between devices  4.75 us (9%)
  between operations  0.65 us (1%)
    all_to_all x1, blocking collectives, shards(): lax.all_to_all(packed, axes, split_axis=0, concat_axis=0, tiled=True)  32.1 us
    all_to_all x1, waiting for transfers between devices, shards(): lax.all_to_all(best.reshape(owners, 2, lanes), axes, split_axis=0, concat...  7.96 us
    all_to_all x1, starting transfers between devices, shards(): lax.all_to_all(best.reshape(owners, 2, lanes), axes, split_axis=0, concat...  4.75 us
    pallas_call x1, Pallas kernels, shards(): pl.pallas_call(score_kernel, out_shape=jax.ShapeDtypeStruct((2 * owners,...  2.6 us
    pallas_call x1, Pallas kernels, shards(): pl.pallas_call(pack_kernel, in_specs=[hbm] * 4, out_shape=(jax.ShapeDtype...  2.44 us
    pallas_call x1, Pallas kernels, shards(): pl.pallas_call(centre_kernel, out_shape=jax.ShapeDtypeStruct((per_owner,...  2.38 us
  transfers between devices with their start and end apart: 1, of which 1 were waited for; matrix products, arithmetic and copies ran while one was open for 0% of the time, Pallas kernels for 4%

profile of v4, /device:TPU:1, one launch (start us, length us, event | category | flops | bytes accessed | tf_op | source)
XLA Modules:
  0.0 53.7 jit_solution(9842644716793163371)
XLA Ops:
  0.6 2.4 %pack.1 = (s16[128,2,2432]{2,1,0:T(2,128)(2,1)S(1)}, s32[8,256]{1,0:T(8,128)S(1)}) custom-call(f32[256,768]{1,0:T(8,128)} %rows_hbm.1, s32[1,256]{1,0:T(1,128)} %bitcast.7, s32[1,256]{1,0:T(1,128)} %bitcast.8, s32[1,256]{1,0:T(1,128)} %bitcast.9), custom_call_target="tpu_custom_call" | custom-call | tf_op jit(solution)/shard_map/pack/pallas_call | solution.py:250
  3.1 32.1 %all_to_all.10.got_ref = s16[128,2,2432]{2,1,0:T(2,128)(2,1)S(1)} all-to-all(s16[128,2,2432]{2,1,0:T(2,128)(2,1)S(1)} %get-tuple-element.4), channel_id=1, replica_groups=mesh['shard'=8,'member'=16] {'shard','member'}, dimensions={0} | all-to-all | bytes 2490368 | tf_op jit(solution)/shard_map/all_to_all | solution.py:277
  35.2 2.6 %score.1 = f32[256,128]{1,0:T(8,128)} custom-call(s16[128,2,2432]{2,1,0:T(2,128)(2,1)S(1)} %all_to_all.10.got_ref), custom_call_target="tpu_custom_call" | custom-call | tf_op jit(solution)/shard_map/score/pallas_call | solution.py:278
  37.8 4.7 %all-to-all-start.1 = ((f32[128,2,128]{2,1,0:T(2,128)}), f32[128,2,128]{2,1,0:T(2,128)S(1)}, u32[]{:S(2)}, u32[]{:S(2)}) async-start(f32[128,2,128]{2,1,0:T(2,128)} %bitcast.3), calls=%async_computation.1 | async-start | bytes 262144 | tf_op jit(solution)/shard_map/all_to_all | solution.py:293
  42.5 2.4 %centre.1 = f32[2,768]{1,0:T(2,128)} custom-call(s16[128,2,2432]{2,1,0:T(2,128)(2,1)S(1)} %all_to_all.10.got_ref), custom_call_target="tpu_custom_call" | custom-call | flops 200000000 | bytes 1300000 | tf_op jit(solution)/shard_map/centre/pallas_call | solution.py:284
  44.9 8.0 %all-to-all-done.1 = f32[128,2,128]{2,1,0:T(2,128)S(1)} async-done(((f32[128,2,128]{2,1,0:T(2,128)}), f32[128,2,128]{2,1,0:T(2,128)S(1)}, u32[]{:S(2)}, u32[]{:S(2)}) %all-to-all-start.1) | async-done | bytes 131104 | tf_op jit(solution)/shard_map/all_to_all | solution.py:293
  52.8 0.8 %unpack.1 = f32[1,256]{1,0:T(1,128)} custom-call(f32[256,128]{1,0:T(8,128)S(1)} %bitcast.6, s32[8,256]{1,0:T(8,128)S(1)} %get-tuple-element.5.route_ref), custom_call_target="tpu_custom_call" | custom-call | tf_op jit(solution)/shard_map/unpack/pallas_call | solution.py:296
Async XLA Ops:
  37.8 15.1 %all-to-all-start.1 = ((f32[128,2,128]{2,1,0:T(2,128)}), f32[128,2,128]{2,1,0:T(2,128)S(1)}, u32[]{:S(2)}, u32[]{:S(2)}) async-start(f32[128,2,128]{2,1,0:T(2,128)} %bitcast.3), calls=%async_computation.1 | async-start | bytes 262144 | tf_op jit(solution)/shard_map/all_to_all | solution.py:293

commit v5 on v4

v5 whole, which is shorter than its diff:
```python
import jax
import jax.numpy as jnp
from jax import lax
from jax.experimental import pallas as pl
from jax.experimental.pallas import tpu as pltpu
from jax.sharding import PartitionSpec as P

epsilon = 1e-06
axes = ("shard", "member")
pairs = 3
slots = 2 * pairs
lanes = 128
id_base = 256
id_range = 32768
full = 32767.0
fields = 16
norm_unit = 256
norm_bytes = 6
f32 = jnp.float32
bf16 = jnp.bfloat16
i32 = jnp.int32
low_half = 0xFFFF
params = pltpu.CompilerParams(vmem_limit_bytes=24 << 20)


def iota(shape, dim):
    return lax.broadcasted_iota(i32, shape, dim)


def dot(a, b, contract=((1,), (0,))):
    return lax.dot_general(a, b, (contract, ((), ())), preferred_element_type=f32)


def one_hot(mask):
    return jnp.where(mask, 1.0, 0.0).astype(bf16)


def count(mask):
    return jnp.sum(jnp.where(mask, 1.0, 0.0), axis=0, keepdims=True)


def to_bytes(values, unit, n):
    digits = []
    rest = values * (1.0 / unit)
    for _ in range(n):
        digit = jnp.floor(rest)
        digits.append(digit)
        rest = (rest - digit) * id_base
    return digits


def pack_kernel(
    rows_hbm,
    clusters_hbm,
    ids_hbm,
    owners_hbm,
    sent_ref,
    route_ref,
    rows_ref,
    clusters_ref,
    ids_ref,
    owners_ref,
    sems,
):
    index_copies = (
        pltpu.make_async_copy(owners_hbm, owners_ref, sems.at[0]),
        pltpu.make_async_copy(clusters_hbm, clusters_ref, sems.at[1]),
        pltpu.make_async_copy(ids_hbm, ids_ref, sems.at[2]),
    )
    copy = pltpu.make_async_copy(rows_hbm, rows_ref, sems.at[3])
    for index_copy in index_copies:
        index_copy.start()
    copy.start()
    for index_copy in index_copies:
        index_copy.wait()
    clusters = clusters_ref[...]
    ids = ids_ref[...]
    owner_map = owners_ref[...].astype(f32)
    row_count, width = rows_ref.shape
    tiles = pairs * (width // lanes) + 1
    owners = sent_ref.shape[0] // tiles
    cluster_count = owner_map.shape[1]

    square = (cluster_count, cluster_count)
    diagonal = iota(square, 0) == iota(square, 1)
    before = iota(square, 0) < iota(square, 1)
    spread = jnp.where(diagonal, owner_map, 0.0).astype(bf16)
    map_col = dot(spread, jnp.ones(square, bf16))
    rank_map = count(before & (map_col == owner_map))
    sub = iota((8, cluster_count), 0)
    table = jnp.where(sub == 0, owner_map, jnp.where(sub == 1, rank_map, 0.0)).astype(bf16)
    cluster_hot = one_hot(iota((cluster_count, row_count), 0) == clusters)
    found = dot(table, cluster_hot)
    owner_col = dot(cluster_hot, map_col[:, :row_count].astype(bf16), ((0,), (0,)))
    slot = count(before & (owner_col == found[0:1])).astype(i32)
    owner = found[0:1].astype(i32)
    rank = found[1:2].astype(i32)

    copy.wait()
    rows = rows_ref[...]
    power = jnp.sum(rows * rows, axis=1, keepdims=True) + epsilon
    inverse = lax.rsqrt(power)
    norm = power * inverse
    largest = jnp.max(jnp.abs(rows), axis=1, keepdims=True) * inverse
    step = jnp.clip(jnp.ceil(largest * full), 1.0, full)
    codes = jnp.floor(rows * (inverse * (full * full / step)) + 0.5)
    upper = codes.astype(bf16)
    halves = jnp.concatenate([upper, (codes - upper.astype(f32)).astype(bf16)], axis=0)
    norm_row = jnp.sum(jnp.where(diagonal, norm, 0.0), axis=0, keepdims=True)
    step_row = jnp.sum(jnp.where(diagonal, step, 0.0), axis=0, keepdims=True)

    values = to_bytes(ids.astype(f32), id_base, 2)
    values = values + [(rank + 1).astype(f32)]
    values = values + to_bytes(step_row, id_base, 2)
    values = values + to_bytes(norm_row, norm_unit, norm_bytes)
    lane = iota((lanes, row_count), 0)
    field = jnp.where(lane // fields == slot, lane % fields, -1)
    notes = jnp.zeros((lanes, row_count), f32)
    for k, value in enumerate(values):
        notes = jnp.where(field == k, value, notes)
    notes = notes.astype(bf16)

    mine = iota((owners, row_count), 0) == owner
    takes = []
    for s in range(slots):
        take = one_hot(mine & (slot == s))
        takes.append(jnp.concatenate([take, take], axis=1))
    placed = dot(jnp.concatenate(takes, axis=0), halves).astype(i32)
    for p in range(pairs):
        even = placed[2 * p * owners : (2 * p + 1) * owners]
        odd = placed[(2 * p + 1) * owners : (2 * p + 2) * owners]
        words = (odd << 16) | (even & low_half)
        for t in range(width // lanes):
            tile = p * (width // lanes) + t
            sent_ref[pl.ds(tile, owners, tiles), :] = words[:, t * lanes : (t + 1) * lanes]
    words = dot(one_hot(mine), notes, ((1,), (1,))).astype(i32)
    sent_ref[pl.ds(tiles - 1, owners, tiles), :] = words
    sub = iota(route_ref.shape, 0)
    route_ref[...] = jnp.where(sub == 0, owner, slot)


def read_tile(got_ref, tile):
    return got_ref[pl.ds(tile, lanes, got_ref.shape[0] // lanes), :]


def read_notes(got_ref):
    return read_tile(got_ref, got_ref.shape[0] // lanes - 1).astype(f32).astype(bf16)


def read_rows(got_ref, p, steps):
    tiles = (got_ref.shape[0] // lanes - 1) // pairs
    even_step = steps[2 * p] * (1.0 / (65536.0 * full * full))
    odd_step = steps[2 * p + 1] * (1.0 / (full * full))
    even = []
    odd = []
    for t in range(tiles):
        words = read_tile(got_ref, p * tiles + t)
        even.append((words << 16).astype(f32) * even_step)
        odd.append((words >> 16).astype(f32) * odd_step)
    return [jnp.concatenate(even, axis=1), jnp.concatenate(odd, axis=1)]


def along_sublanes(notes, first, third):
    sub = iota((lanes, lanes), 0)
    field = sub % fields
    weight = jnp.where(field == first, float(id_base), 0.0)
    weight = jnp.where(field == first + 1, 1.0, weight)
    if third is not None:
        weight = jnp.where(field == third, float(id_range), weight)
    of = sub // fields
    spread = [jnp.where(of == s, weight, 0.0).astype(bf16) for s in range(slots)]
    tall = dot(notes, jnp.concatenate(spread, axis=1))
    return [tall[:, s * lanes : (s + 1) * lanes] for s in range(slots)]


def score_kernel(got_ref, best_ref):
    owners = lanes
    total = slots * owners
    notes = read_notes(got_ref)
    sub = iota((8 * slots, lanes), 0)
    field = iota((8 * slots, lanes), 1) - fields * (sub // 8)
    kind = sub % 8
    pick = jnp.where((kind == 0) & (field == 0), float(id_base), 0.0)
    pick = jnp.where((kind == 0) & (field == 1), 1.0, pick)
    pick = jnp.where((kind == 0) & (field == 2), float(id_range), pick)
    pick = jnp.where((kind == 1) & (field == 2), 1.0, pick)
    wide = dot(pick.astype(bf16), notes, ((1,), (1,)))
    high = jnp.concatenate([wide[8 * s : 8 * s + 1] for s in range(slots)], axis=1)
    low = jnp.concatenate([wide[8 * s + 1 : 8 * s + 2] for s in range(slots)], axis=1)
    low = low * float(id_range)
    key = jnp.concatenate(along_sublanes(notes, 0, 2), axis=0)
    step = along_sublanes(notes, 3, None)
    keys = []
    for p in range(pairs):
        keys = keys + [rows.astype(bf16) for rows in read_rows(got_ref, p, step)]
    keys = jnp.concatenate(keys, axis=0)

    block = 2 * lanes
    other = jnp.concatenate([key] * (block // lanes), axis=1)
    bests = []
    for start in range(0, total, block):
        stop = start + block
        scores = dot(keys, keys[start:stop], ((1,), (1,)))
        allowed = (other >= low[:, start:stop]) & (other < high[:, start:stop])
        bests.append(jnp.max(jnp.where(allowed, scores, -1.0), axis=0, keepdims=True))
    best = jnp.concatenate(bests, axis=1)
    sub = iota((lanes, owners), 0)
    rows = jnp.full((lanes, owners), -1.0, f32)
    for s in range(slots):
        rows = jnp.where(sub == s, best[:, s * owners : (s + 1) * owners], rows)
    best_ref[...] = rows.T


def centre_kernel(got_ref, sums_ref):
    owned, width = sums_ref.shape
    owners = lanes
    notes = read_notes(got_ref)
    sub = iota((8 * slots, lanes), 0)
    field = iota((8 * slots, lanes), 1) - fields * (sub // 8)
    kind = sub % 8
    pick = jnp.where((kind == 1) & (field == 2), 1.0, 0.0)
    for k in range(norm_bytes):
        weight = float(norm_unit) / float(id_base) ** k
        pick = jnp.where((kind == 0) & (field == 5 + k), weight, pick)
    wide = dot(pick.astype(bf16), notes, ((1,), (1,)))
    step = along_sublanes(notes, 3, None)

    sub = iota((8, owners), 0)
    sums = jnp.zeros((8, width), f32)
    for p in range(pairs):
        exact = jnp.concatenate(read_rows(got_ref, p, step), axis=0)
        unit = exact.astype(bf16)
        rest = (exact - unit.astype(f32)).astype(bf16)
        weights = []
        for s in (2 * p, 2 * p + 1):
            norms = wide[8 * s : 8 * s + 1]
            ranks = wide[8 * s + 1 : 8 * s + 2]
            coarse = norms.astype(bf16).astype(f32)
            weight = jnp.where(sub < owned, coarse, norms - coarse)
            weight = jnp.where(ranks == (sub % owned + 1).astype(f32), weight, 0.0)
            weights.append(jnp.where(sub < 2 * owned, weight, 0.0).astype(bf16))
        weight = jnp.concatenate(weights, axis=1)
        sums = sums + dot(weight, unit) + dot(weight, rest)
    sums = sums[0:owned] + sums[owned : 2 * owned]
    scale = lax.rsqrt(jnp.mean(sums * sums, axis=1, keepdims=True) + epsilon)
    sums_ref[...] = sums * scale


def exact_dot(values, hot, contract=((1,), (0,))):
    first = values.astype(bf16)
    rest = values - first.astype(f32)
    second = rest.astype(bf16)
    third = (rest - second.astype(f32)).astype(bf16)
    return dot(first, hot, contract) + dot(second, hot, contract) + dot(third, hot, contract)


def unpack_kernel(back_ref, route_ref, out_ref):
    owner = route_ref[0:1, :]
    slot = route_ref[1:2, :]
    back = back_ref[...]
    row_count = owner.shape[1]
    hot = one_hot(iota((back.shape[0], row_count), 0) == owner)
    found = exact_dot(back, hot, ((0,), (0,)))[0:8]
    mine = iota((8, row_count), 0) == slot
    out_ref[...] = jnp.sum(jnp.where(mine, found, 0.0), axis=0, keepdims=True)


def shards(embeddings, clusters, row_ids, owner_map):
    owners = lax.axis_size("shard") * lax.axis_size("member")
    local_rows, width = embeddings.shape
    cluster_count = owner_map.shape[0]
    per_owner = cluster_count // owners
    tiles = pairs * (width // lanes) + 1
    hbm = pl.BlockSpec(memory_space=pltpu.HBM)
    packed, route = pl.pallas_call(
        pack_kernel,
        in_specs=[hbm] * 4,
        out_shape=(
            jax.ShapeDtypeStruct((owners * tiles, lanes), i32),
            jax.ShapeDtypeStruct((8, local_rows), i32),
        ),
        scratch_shapes=[
            pltpu.VMEM((local_rows, width), f32),
            pltpu.VMEM((1, local_rows), i32),
            pltpu.VMEM((1, local_rows), i32),
            pltpu.VMEM((1, cluster_count), i32),
            pltpu.SemaphoreType.DMA((4,)),
        ],
        compiler_params=params,
        name="pack",
    )(
        *[
            pltpu.with_memory_space_constraint(x, pltpu.HBM)
            for x in (
                embeddings,
                clusters.reshape(1, local_rows),
                row_ids.reshape(1, local_rows),
                owner_map.reshape(1, cluster_count),
            )
        ]
    )
    packed = packed.reshape(owners, tiles, 1, lanes)
    received = lax.all_to_all(packed, axes, split_axis=0, concat_axis=0, tiled=True)
    received = received.reshape(owners * tiles, lanes)
    best = pl.pallas_call(
        score_kernel,
        out_shape=jax.ShapeDtypeStruct((owners, lanes), f32),
        compiler_params=params,
        name="score",
    )(received)
    centroids = pl.pallas_call(
        centre_kernel,
        out_shape=jax.ShapeDtypeStruct((per_owner, width), f32),
        cost_estimate=pl.CostEstimate(
            flops=200_000_000, bytes_accessed=1_300_000, transcendentals=0
        ),
        compiler_params=params,
        name="centre",
    )(received)
    returned = lax.all_to_all(
        best.reshape(owners, 1, lanes), axes, split_axis=0, concat_axis=0, tiled=True
    )
    earlier_max = pl.pallas_call(
        unpack_kernel,
        out_shape=jax.ShapeDtypeStruct((1, local_rows), f32),
        compiler_params=params,
        name="unpack",
    )(returned.reshape(owners, lanes), route)
    return (centroids, earlier_max.reshape(local_rows))


def solution(mesh):
    placed = (P(axes, None), P(axes), P(axes), P())
    return jax.shard_map(
        shards,
        mesh=mesh,
        in_specs=placed,
        out_specs=(P(axes, None), P(axes)),
        check_vma=False,
    )
```

time: 53.8 us -> 52.8 us (0.981)
  Pallas kernels: 8.23 us -> 6.65 us
    pallas_call x1, Pallas kernels: 2.38 us -> 1.48 us  [shards(): pl.pallas_call(centre_kernel, out_shape=jax.ShapeDtypeStruct((per_owner,...]
  transfers between devices with their start and end apart: 1 -> 1, of which waited for: 1 -> 1; matrix products, arithmetic and copies ran while one was open for 0% -> 0% of each run, Pallas kernels for 4% -> 3%
where the time goes in v5:
time: 52.8 us; the launch traced here: 52.6 us
  blocking collectives  32.1 us (61%)
  waiting for transfers between devices  8.46 us (16%)
  Pallas kernels  6.65 us (13%)
  starting transfers between devices  4.74 us (9%)
  between operations  0.65 us (1%)
    all_to_all x1, blocking collectives, shards(): lax.all_to_all(packed, axes, split_axis=0, concat_axis=0, tiled=True)  32.1 us
    all_to_all x1, waiting for transfers between devices, shards(): lax.all_to_all(best.reshape(owners, 1, lanes), axes, split_axis=0, concat...  8.46 us
    all_to_all x1, starting transfers between devices, shards(): lax.all_to_all(best.reshape(owners, 1, lanes), axes, split_axis=0, concat...  4.74 us
    pallas_call x1, Pallas kernels, shards(): pl.pallas_call(pack_kernel, in_specs=[hbm] * 4, out_shape=(jax.ShapeDtype...  2.23 us
    pallas_call x1, Pallas kernels, shards(): pl.pallas_call(score_kernel, out_shape=jax.ShapeDtypeStruct((owners, lane...  2.16 us
    pallas_call x1, Pallas kernels, shards(): pl.pallas_call(centre_kernel, out_shape=jax.ShapeDtypeStruct((per_owner,...  1.48 us
  transfers between devices with their start and end apart: 1, of which 1 were waited for; matrix products, arithmetic and copies ran while one was open for 0% of the time, Pallas kernels for 3%

profile of v5, /device:TPU:1, one launch (start us, length us, event | category | flops | bytes accessed | tf_op | source)
XLA Modules:
  0.0 52.6 jit_solution(6444746004843856579)
XLA Ops:
  0.6 2.2 %pack.1 = (s32[2432,128]{1,0:T(8,128)S(1)}, s32[8,256]{1,0:T(8,128)S(1)}) custom-call(f32[256,768]{1,0:T(8,128)} %rows_hbm.1, s32[1,256]{1,0:T(1,128)} %bitcast.14, s32[1,256]{1,0:T(1,128)} %bitcast.15, s32[1,256]{1,0:T(1,128)} %bitcast.16), custom_call_target="tpu_custom_call" | custom-call | tf_op jit(solution)/shard_map/pack/pallas_call | solution.py:275
  2.9 32.1 %all_to_all.10 = s32[128,19,1,128]{3,2,1,0:T(1,128)S(1)} all-to-all(s32[128,19,1,128]{3,2,1,0:T(1,128)S(1)} %bitcast.12), channel_id=1, replica_groups=mesh['shard'=8,'member'=16] {'shard','member'}, dimensions={0} | all-to-all | bytes 2490368 | tf_op jit(solution)/shard_map/all_to_all | solution.py:303
  34.9 2.2 %score.1 = f32[128,128]{1,0:T(8,128)} custom-call(s32[2432,128]{1,0:T(8,128)S(1)} %bitcast.10), custom_call_target="tpu_custom_call" | custom-call | tf_op jit(solution)/shard_map/score/pallas_call | solution.py:305
  37.1 4.7 %all-to-all-start.1 = ((f32[128,1,128]{2,1,0:T(1,128)}), f32[128,1,128]{2,1,0:T(1,128)S(1)}, u32[]{:S(2)}, u32[]{:S(2)}) async-start(f32[128,1,128]{2,1,0:T(1,128)} %bitcast.6), calls=%async_computation.1 | async-start | bytes 131072 | tf_op jit(solution)/shard_map/all_to_all | solution.py:320
  41.9 1.5 %centre.1 = f32[2,768]{1,0:T(2,128)} custom-call(s32[2432,128]{1,0:T(8,128)S(1)} %bitcast.11), custom_call_target="tpu_custom_call" | custom-call | flops 200000000 | bytes 1300000 | tf_op jit(solution)/shard_map/centre/pallas_call | solution.py:311
  43.3 8.5 %all-to-all-done.1 = f32[128,1,128]{2,1,0:T(1,128)S(1)} async-done(((f32[128,1,128]{2,1,0:T(1,128)}), f32[128,1,128]{2,1,0:T(1,128)S(1)}, u32[]{:S(2)}, u32[]{:S(2)}) %all-to-all-start.1) | async-done | bytes 65568 | tf_op jit(solution)/shard_map/all_to_all | solution.py:320
  51.8 0.8 %unpack.1 = f32[1,256]{1,0:T(1,128)} custom-call(f32[128,128]{1,0:T(8,128)S(1)} %bitcast.13, s32[8,256]{1,0:T(8,128)S(1)} %get-tuple-element.5.route_ref), custom_call_target="tpu_custom_call" | custom-call | tf_op jit(solution)/shard_map/unpack/pallas_call | solution.py:323
Async XLA Ops:
  37.1 14.7 %all-to-all-start.1 = ((f32[128,1,128]{2,1,0:T(1,128)}), f32[128,1,128]{2,1,0:T(1,128)S(1)}, u32[]{:S(2)}, u32[]{:S(2)}) async-start(f32[128,1,128]{2,1,0:T(1,128)} %bitcast.6), calls=%async_computation.1 | async-start | bytes 131072 | tf_op jit(solution)/shard_map/all_to_all | solution.py:320

commit v6 on v5

--- a/solution.py
+++ b/solution.py
@@ -173,9 +173,10 @@
     return [tall[:, s * lanes : (s + 1) * lanes] for s in range(slots)]
 
 
-def score_kernel(got_ref, best_ref):
+def score_kernel(got_ref, sums_hbm, best_ref, sums_ref, sem):
     owners = lanes
     total = slots * owners
+    owned, width = sums_ref.shape
     notes = read_notes(got_ref)
     sub = iota((8 * slots, lanes), 0)
     field = iota((8 * slots, lanes), 1) - fields * (sub // 8)
@@ -184,16 +185,36 @@
     pick = jnp.where((kind == 0) & (field == 1), 1.0, pick)
     pick = jnp.where((kind == 0) & (field == 2), float(id_range), pick)
     pick = jnp.where((kind == 1) & (field == 2), 1.0, pick)
+    for k in range(norm_bytes):
+        weight = float(norm_unit) / float(id_base) ** k
+        pick = jnp.where((kind == 2) & (field == 5 + k), weight, pick)
     wide = dot(pick.astype(bf16), notes, ((1,), (1,)))
-    high = jnp.concatenate([wide[8 * s : 8 * s + 1] for s in range(slots)], axis=1)
-    low = jnp.concatenate([wide[8 * s + 1 : 8 * s + 2] for s in range(slots)], axis=1)
-    low = low * float(id_range)
+    line = [
+        jnp.concatenate([wide[8 * s + k : 8 * s + k + 1] for s in range(slots)], axis=1)
+        for k in range(3)
+    ]
+    high = line[0]
+    low = line[1] * float(id_range)
     key = jnp.concatenate(along_sublanes(notes, 0, 2), axis=0)
     step = along_sublanes(notes, 3, None)
-    keys = []
+    exact = []
     for p in range(pairs):
-        keys = keys + [rows.astype(bf16) for rows in read_rows(got_ref, p, step)]
-    keys = jnp.concatenate(keys, axis=0)
+        exact = exact + read_rows(got_ref, p, step)
+    exact = jnp.concatenate(exact, axis=0)
+    keys = exact.astype(bf16)
+    rest = (exact - keys.astype(f32)).astype(bf16)
+
+    sub = iota((8, total), 0)
+    coarse = line[2].astype(bf16).astype(f32)
+    weight = jnp.where(sub < owned, coarse, line[2] - coarse)
+    weight = jnp.where(line[1] == (sub % owned + 1).astype(f32), weight, 0.0)
+    weight = jnp.where(sub < 2 * owned, weight, 0.0).astype(bf16)
+    sums = dot(weight, keys) + dot(weight, rest)
+    sums = sums[0:owned] + sums[owned : 2 * owned]
+    scale = lax.rsqrt(jnp.mean(sums * sums, axis=1, keepdims=True) + epsilon)
+    sums_ref[...] = sums * scale
+    copy = pltpu.make_async_copy(sums_ref, sums_hbm, sem)
+    copy.start()
 
     block = 2 * lanes
     other = jnp.concatenate([key] * (block // lanes), axis=1)
@@ -209,41 +230,7 @@
     for s in range(slots):
         rows = jnp.where(sub == s, best[:, s * owners : (s + 1) * owners], rows)
     best_ref[...] = rows.T
-
-
-def centre_kernel(got_ref, sums_ref):
-    owned, width = sums_ref.shape
-    owners = lanes
-    notes = read_notes(got_ref)
-    sub = iota((8 * slots, lanes), 0)
-    field = iota((8 * slots, lanes), 1) - fields * (sub // 8)
-    kind = sub % 8
-    pick = jnp.where((kind == 1) & (field == 2), 1.0, 0.0)
-    for k in range(norm_bytes):
-        weight = float(norm_unit) / float(id_base) ** k
-        pick = jnp.where((kind == 0) & (field == 5 + k), weight, pick)
-    wide = dot(pick.astype(bf16), notes, ((1,), (1,)))
-    step = along_sublanes(notes, 3, None)
-
-    sub = iota((8, owners), 0)
-    sums = jnp.zeros((8, width), f32)
-    for p in range(pairs):
-        exact = jnp.concatenate(read_rows(got_ref, p, step), axis=0)
-        unit = exact.astype(bf16)
-        rest = (exact - unit.astype(f32)).astype(bf16)
-        weights = []
-        for s in (2 * p, 2 * p + 1):
-            norms = wide[8 * s : 8 * s + 1]
-            ranks = wide[8 * s + 1 : 8 * s + 2]
-            coarse = norms.astype(bf16).astype(f32)
-            weight = jnp.where(sub < owned, coarse, norms - coarse)
-            weight = jnp.where(ranks == (sub % owned + 1).astype(f32), weight, 0.0)
-            weights.append(jnp.where(sub < 2 * owned, weight, 0.0).astype(bf16))
-        weight = jnp.concatenate(weights, axis=1)
-        sums = sums + dot(weight, unit) + dot(weight, rest)
-    sums = sums[0:owned] + sums[owned : 2 * owned]
-    scale = lax.rsqrt(jnp.mean(sums * sums, axis=1, keepdims=True) + epsilon)
-    sums_ref[...] = sums * scale
+    copy.wait()
 
 
 def exact_dot(values, hot, contract=((1,), (0,))):
@@ -302,20 +289,16 @@
     packed = packed.reshape(owners, tiles, 1, lanes)
     received = lax.all_to_all(packed, axes, split_axis=0, concat_axis=0, tiled=True)
     received = received.reshape(owners * tiles, lanes)
-    best = pl.pallas_call(
+    centroids, best = pl.pallas_call(
         score_kernel,
-        out_shape=jax.ShapeDtypeStruct((owners, lanes), f32),
+        out_shape=(
+            jax.ShapeDtypeStruct((per_owner, width), f32),
+            jax.ShapeDtypeStruct((owners, lanes), f32),
+        ),
+        out_specs=(hbm, pl.BlockSpec(memory_space=pltpu.VMEM)),
+        scratch_shapes=[pltpu.VMEM((per_owner, width), f32), pltpu.SemaphoreType.DMA(())],
         compiler_params=params,
         name="score",
-    )(received)
-    centroids = pl.pallas_call(
-        centre_kernel,
-        out_shape=jax.ShapeDtypeStruct((per_owner, width), f32),
-        cost_estimate=pl.CostEstimate(
-            flops=200_000_000, bytes_accessed=1_300_000, transcendentals=0
-        ),
-        compiler_params=params,
-        name="centre",
     )(received)
     returned = lax.all_to_all(
         best.reshape(owners, 1, lanes), axes, split_axis=0, concat_axis=0, tiled=True

time: 52.8 us -> 52 us (0.985)
  blocking collectives: 32.1 us -> 46.1 us
  waiting for transfers between devices: 8.46 us -> 0 us
  starting transfers between devices: 4.74 us -> 0 us
  Pallas kernels: 6.65 us -> 5.05 us
    all_to_all x0 -> x1, blocking collectives: none -> 14.1 us  [shards(): lax.all_to_all(best.reshape(owners, 1, lanes), axes, split_axis=0, concat...]
    all_to_all x1 -> x0, waiting for transfers between devices: 8.46 us -> none  [shards(): lax.all_to_all(best.reshape(owners, 1, lanes), axes, split_axis=0, concat...]
    all_to_all x1 -> x0, starting transfers between devices: 4.74 us -> none  [shards(): lax.all_to_all(best.reshape(owners, 1, lanes), axes, split_axis=0, concat...]
    pallas_call x2 -> x1, Pallas kernels: 3.65 us -> 2.05 us  [shards(): pl.pallas_call(score_kernel, out_shape=(jax.ShapeDtypeStruct((per_owner,...]
  transfers between devices with their start and end apart: 1 -> 0, of which waited for: 1 -> 0; matrix products, arithmetic and copies ran while one was open for 0% -> 0% of each run, Pallas kernels for 3% -> 0%
where the time goes in v6:
time: 52 us; the launch traced here: 51.8 us
  blocking collectives  46.1 us (89%)
  Pallas kernels  5.05 us (10%)
  between operations  0.65 us (1%)
    all_to_all x1, blocking collectives, shards(): lax.all_to_all(packed, axes, split_axis=0, concat_axis=0, tiled=True)  32.1 us
    all_to_all x1, blocking collectives, shards(): lax.all_to_all(best.reshape(owners, 1, lanes), axes, split_axis=0, concat...  14.1 us
    pallas_call x1, Pallas kernels, shards(): pl.pallas_call(pack_kernel, in_specs=[hbm] * 4, out_shape=(jax.ShapeDtype...  2.23 us
    pallas_call x1, Pallas kernels, shards(): pl.pallas_call(score_kernel, out_shape=(jax.ShapeDtypeStruct((per_owner,...  2.05 us

profile of v6, /device:TPU:1, one launch (start us, length us, event | category | flops | bytes accessed | tf_op | source)
XLA Modules:
  0.0 51.8 jit_solution(5962531293595590587)
XLA Ops:
  0.6 2.2 %pack.1 = (s32[2432,128]{1,0:T(8,128)S(1)}, s32[8,256]{1,0:T(8,128)S(1)}) custom-call(f32[256,768]{1,0:T(8,128)} %rows_hbm.1, s32[1,256]{1,0:T(1,128)} %bitcast.14, s32[1,256]{1,0:T(1,128)} %bitcast.15, s32[1,256]{1,0:T(1,128)} %bitcast.16), custom_call_target="tpu_custom_call" | custom-call | tf_op jit(solution)/shard_map/pack/pallas_call | solution.py:262
  2.9 32.1 %all_to_all.10 = s32[128,19,1,128]{3,2,1,0:T(1,128)S(1)} all-to-all(s32[128,19,1,128]{3,2,1,0:T(1,128)S(1)} %bitcast.11), channel_id=1, replica_groups=mesh['shard'=8,'member'=16] {'shard','member'}, dimensions={0} | all-to-all | bytes 2490368 | tf_op jit(solution)/shard_map/all_to_all | solution.py:290
  34.9 2.1 %score.1 = (f32[2,768]{1,0:T(2,128)}, f32[128,128]{1,0:T(8,128)S(1)}) custom-call(s32[2432,128]{1,0:T(8,128)S(1)} %bitcast.10), custom_call_target="tpu_custom_call" | custom-call | tf_op jit(solution)/shard_map/score/pallas_call | solution.py:292
  37.0 14.1 %all_to_all.11 = f32[128,1,128]{2,1,0:T(1,128)S(1)} all-to-all(f32[128,1,128]{2,1,0:T(1,128)S(1)} %bitcast.13), channel_id=1, replica_groups=mesh['shard'=8,'member'=16] {'shard','member'}, dimensions={0} | all-to-all | bytes 131072 | tf_op jit(solution)/shard_map/all_to_all | solution.py:303
  51.1 0.8 %unpack.1 = f32[1,256]{1,0:T(1,128)} custom-call(f32[128,128]{1,0:T(8,128)S(1)} %bitcast.12, s32[8,256]{1,0:T(8,128)S(1)} %get-tuple-element.9.route_ref), custom_call_target="tpu_custom_call" | custom-call | tf_op jit(solution)/shard_map/unpack/pallas_call | solution.py:306

commit v7 on v6

--- a/solution.py
+++ b/solution.py
@@ -1,3 +1,5 @@
+import functools
+
 import jax
 import jax.numpy as jnp
 from jax import lax
@@ -7,6 +9,7 @@
 
 epsilon = 1e-06
 axes = ("shard", "member")
+exchange = ("member", "shard")
 pairs = 3
 slots = 2 * pairs
 lanes = 128
@@ -61,6 +64,8 @@
     ids_ref,
     owners_ref,
     sems,
+    *,
+    members,
 ):
     index_copies = (
         pltpu.make_async_copy(owners_hbm, owners_ref, sems.at[0]),
@@ -75,7 +80,9 @@
         index_copy.wait()
     clusters = clusters_ref[...]
     ids = ids_ref[...]
-    owner_map = owners_ref[...].astype(f32)
+    owner_map = owners_ref[...]
+    owner_map = owner_map % members * (lanes // members) + owner_map // members
+    owner_map = owner_map.astype(f32)
     row_count, width = rows_ref.shape
     tiles = pairs * (width // lanes) + 1
     owners = sent_ref.shape[0] // tiles
@@ -109,7 +116,8 @@
     norm_row = jnp.sum(jnp.where(diagonal, norm, 0.0), axis=0, keepdims=True)
     step_row = jnp.sum(jnp.where(diagonal, step, 0.0), axis=0, keepdims=True)
 
-    values = to_bytes(ids.astype(f32), id_base, 2)
+    side = (2 * rank - 1).astype(f32)
+    values = [side * digit for digit in to_bytes((id_range - ids).astype(f32), id_base, 2)]
     values = values + [(rank + 1).astype(f32)]
     values = values + to_bytes(step_row, id_base, 2)
     values = values + to_bytes(norm_row, norm_unit, norm_bytes)
@@ -160,13 +168,11 @@
     return [jnp.concatenate(even, axis=1), jnp.concatenate(odd, axis=1)]
 
 
-def along_sublanes(notes, first, third):
+def along_sublanes(notes, first):
     sub = iota((lanes, lanes), 0)
     field = sub % fields
     weight = jnp.where(field == first, float(id_base), 0.0)
     weight = jnp.where(field == first + 1, 1.0, weight)
-    if third is not None:
-        weight = jnp.where(field == third, float(id_range), weight)
     of = sub // fields
     spread = [jnp.where(of == s, weight, 0.0).astype(bf16) for s in range(slots)]
     tall = dot(notes, jnp.concatenate(spread, axis=1))
@@ -183,7 +189,6 @@
     kind = sub % 8
     pick = jnp.where((kind == 0) & (field == 0), float(id_base), 0.0)
     pick = jnp.where((kind == 0) & (field == 1), 1.0, pick)
-    pick = jnp.where((kind == 0) & (field == 2), float(id_range), pick)
     pick = jnp.where((kind == 1) & (field == 2), 1.0, pick)
     for k in range(norm_bytes):
         weight = float(norm_unit) / float(id_base) ** k
@@ -193,10 +198,10 @@
         jnp.concatenate([wide[8 * s + k : 8 * s + k + 1] for s in range(slots)], axis=1)
         for k in range(3)
     ]
-    high = line[0]
-    low = line[1] * float(id_range)
-    key = jnp.concatenate(along_sublanes(notes, 0, 2), axis=0)
-    step = along_sublanes(notes, 3, None)
+    side = jnp.where(line[0] > 0.0, 1.0, -1.0)
+    size = jnp.abs(line[0])
+    key = jnp.concatenate(along_sublanes(notes, 0), axis=0)
+    step = along_sublanes(notes, 3)
     exact = []
     for p in range(pairs):
         exact = exact + read_rows(got_ref, p, step)
@@ -204,25 +209,29 @@
     keys = exact.astype(bf16)
     rest = (exact - keys.astype(f32)).astype(bf16)
 
-    sub = iota((8, total), 0)
-    coarse = line[2].astype(bf16).astype(f32)
-    weight = jnp.where(sub < owned, coarse, line[2] - coarse)
-    weight = jnp.where(line[1] == (sub % owned + 1).astype(f32), weight, 0.0)
-    weight = jnp.where(sub < 2 * owned, weight, 0.0).astype(bf16)
-    sums = dot(weight, keys) + dot(weight, rest)
-    sums = sums[0:owned] + sums[owned : 2 * owned]
-    scale = lax.rsqrt(jnp.mean(sums * sums, axis=1, keepdims=True) + epsilon)
-    sums_ref[...] = sums * scale
     copy = pltpu.make_async_copy(sums_ref, sums_hbm, sem)
-    copy.start()
+
+    def centre():
+        sub = iota((8, total), 0)
+        coarse = line[2].astype(bf16).astype(f32)
+        weight = jnp.where(sub < owned, coarse, line[2] - coarse)
+        weight = jnp.where(line[1] == (sub % owned + 1).astype(f32), weight, 0.0)
+        weight = jnp.where(sub < 2 * owned, weight, 0.0).astype(bf16)
+        sums = dot(weight, keys) + dot(weight, rest)
+        sums = sums[0:owned] + sums[owned : 2 * owned]
+        scale = lax.rsqrt(jnp.mean(sums * sums, axis=1, keepdims=True) + epsilon)
+        sums_ref[...] = sums * scale
+        copy.start()
 
     block = 2 * lanes
     other = jnp.concatenate([key] * (block // lanes), axis=1)
     bests = []
     for start in range(0, total, block):
+        if start == 1 * block:
+            centre()
         stop = start + block
         scores = dot(keys, keys[start:stop], ((1,), (1,)))
-        allowed = (other >= low[:, start:stop]) & (other < high[:, start:stop])
+        allowed = other * side[:, start:stop] > size[:, start:stop]
         bests.append(jnp.max(jnp.where(allowed, scores, -1.0), axis=0, keepdims=True))
     best = jnp.concatenate(bests, axis=1)
     sub = iota((lanes, owners), 0)
@@ -260,7 +269,7 @@
     tiles = pairs * (width // lanes) + 1
     hbm = pl.BlockSpec(memory_space=pltpu.HBM)
     packed, route = pl.pallas_call(
-        pack_kernel,
+        functools.partial(pack_kernel, members=lax.axis_size("member")),
         in_specs=[hbm] * 4,
         out_shape=(
             jax.ShapeDtypeStruct((owners * tiles, lanes), i32),
@@ -287,7 +296,7 @@
         ]
     )
     packed = packed.reshape(owners, tiles, 1, lanes)
-    received = lax.all_to_all(packed, axes, split_axis=0, concat_axis=0, tiled=True)
+    received = lax.all_to_all(packed, exchange, split_axis=0, concat_axis=0, tiled=True)
     received = received.reshape(owners * tiles, lanes)
     centroids, best = pl.pallas_call(
         score_kernel,
@@ -301,7 +310,7 @@
         name="score",
     )(received)
     returned = lax.all_to_all(
-        best.reshape(owners, 1, lanes), axes, split_axis=0, concat_axis=0, tiled=True
+        best.reshape(owners, 1, lanes), exchange, split_axis=0, concat_axis=0, tiled=True
     )
     earlier_max = pl.pallas_call(
         unpack_kernel,

time: 52 us -> 52.5 us (level)
  no operation moved by 1% of the time
where the time goes in v7:
time: 52.5 us; the launch traced here: 52.3 us
  blocking collectives  46.4 us (88%)
  Pallas kernels  5.24 us (10%)
  between operations  0.65 us (1%)
    all_to_all x1, blocking collectives, shards(): lax.all_to_all(packed, exchange, split_axis=0, concat_axis=0, tiled=True)  32.6 us
    all_to_all x1, blocking collectives, shards(): lax.all_to_all(best.reshape(owners, 1, lanes), exchange, split_axis=0, co...  13.8 us
    pallas_call x1, Pallas kernels, shards(): pl.pallas_call(score_kernel, out_shape=(jax.ShapeDtypeStruct((per_owner,...  2.24 us
    pallas_call x1, Pallas kernels, shards(): pl.pallas_call(functools.partial(pack_kernel, members=lax.axis_size('memb...  2.23 us

profile of v7, /device:TPU:1, one launch (start us, length us, event | category | flops | bytes accessed | tf_op | source)
XLA Modules:
  0.0 52.3 jit_solution(9397017373774735981)
XLA Ops:
  0.6 2.2 %pack.1 = (s32[2432,128]{1,0:T(8,128)S(1)}, s32[8,256]{1,0:T(8,128)S(1)}) custom-call(f32[256,768]{1,0:T(8,128)} %rows_hbm.1, s32[1,256]{1,0:T(1,128)} %bitcast.14, s32[1,256]{1,0:T(1,128)} %bitcast.15, s32[1,256]{1,0:T(1,128)} %bitcast.16), custom_call_target="tpu_custom_call" | custom-call | tf_op jit(solution)/shard_map/pack/pallas_call | solution.py:271
  2.9 32.6 %all_to_all.10 = s32[128,19,1,128]{3,2,1,0:T(1,128)S(1)} all-to-all(s32[128,19,1,128]{3,2,1,0:T(1,128)S(1)} %bitcast.11), channel_id=1, replica_groups=mesh['shard'=8,'member'=16] {'member','shard'}, dimensions={0} | all-to-all | bytes 2490368 | tf_op jit(solution)/shard_map/all_to_all | solution.py:299
  35.5 2.2 %score.1 = (f32[2,768]{1,0:T(2,128)}, f32[128,128]{1,0:T(8,128)S(1)}) custom-call(s32[2432,128]{1,0:T(8,128)S(1)} %bitcast.10), custom_call_target="tpu_custom_call" | custom-call | tf_op jit(solution)/shard_map/score/pallas_call | solution.py:301
  37.7 13.8 %all_to_all.11 = f32[128,1,128]{2,1,0:T(1,128)S(1)} all-to-all(f32[128,1,128]{2,1,0:T(1,128)S(1)} %bitcast.13), channel_id=1, replica_groups=mesh['shard'=8,'member'=16] {'member','shard'}, dimensions={0} | all-to-all | bytes 131072 | tf_op jit(solution)/shard_map/all_to_all | solution.py:312
  51.5 0.8 %unpack.1 = f32[1,256]{1,0:T(1,128)} custom-call(f32[128,128]{1,0:T(8,128)S(1)} %bitcast.12, s32[8,256]{1,0:T(8,128)S(1)} %get-tuple-element.9.route_ref), custom_call_target="tpu_custom_call" | custom-call | tf_op jit(solution)/shard_map/unpack/pallas_call | solution.py:315

commit v8 on v7

--- a/solution.py
+++ b/solution.py
@@ -9,10 +9,10 @@
 
 epsilon = 1e-06
 axes = ("shard", "member")
-exchange = ("member", "shard")
 pairs = 3
 slots = 2 * pairs
 lanes = 128
+half = 64
 id_base = 256
 id_range = 32768
 full = 32767.0
@@ -80,9 +80,7 @@
         index_copy.wait()
     clusters = clusters_ref[...]
     ids = ids_ref[...]
-    owner_map = owners_ref[...]
-    owner_map = owner_map % members * (lanes // members) + owner_map // members
-    owner_map = owner_map.astype(f32)
+    owner_map = owners_ref[...].astype(f32)
     row_count, width = rows_ref.shape
     tiles = pairs * (width // lanes) + 1
     owners = sent_ref.shape[0] // tiles
@@ -128,7 +126,9 @@
         notes = jnp.where(field == k, value, notes)
     notes = notes.astype(bf16)
 
-    mine = iota((owners, row_count), 0) == owner
+    chip = owner // (2 * members) * members + owner % members
+    other = owner // members % 2 != lax.axis_index("shard") % 2
+    mine = iota((owners, row_count), 0) == 2 * chip + jnp.where(other, 1, 0)
     takes = []
     for s in range(slots):
         take = one_hot(mine & (slot == s))
@@ -147,22 +147,32 @@
     route_ref[...] = jnp.where(sub == 0, owner, slot)
 
 
-def read_tile(got_ref, tile):
-    return got_ref[pl.ds(tile, lanes, got_ref.shape[0] // lanes), :]
-
-
-def read_notes(got_ref):
-    return read_tile(got_ref, got_ref.shape[0] // lanes - 1).astype(f32).astype(bf16)
-
-
-def read_rows(got_ref, p, steps):
-    tiles = (got_ref.shape[0] // lanes - 1) // pairs
+def split_kernel(got_ref, other_ref):
+    tiles = other_ref.shape[0] // half
+    for t in range(tiles):
+        words = got_ref[pl.ds(tiles + t, half, 2 * tiles), :]
+        other_ref[pl.ds(t, half, tiles), :] = words
+
+
+def read_tile(got_refs, tile):
+    mine_ref, other_ref = got_refs
+    tiles = other_ref.shape[0] // half
+    mine = mine_ref[pl.ds(tile, half, 2 * tiles), :]
+    return jnp.concatenate([mine, other_ref[pl.ds(tile, half, tiles), :]], axis=0)
+
+
+def read_notes(got_refs):
+    return read_tile(got_refs, got_refs[1].shape[0] // half - 1).astype(f32).astype(bf16)
+
+
+def read_rows(got_refs, p, steps):
+    tiles = (got_refs[1].shape[0] // half - 1) // pairs
     even_step = steps[2 * p] * (1.0 / (65536.0 * full * full))
     odd_step = steps[2 * p + 1] * (1.0 / (full * full))
     even = []
     odd = []
     for t in range(tiles):
-        words = read_tile(got_ref, p * tiles + t)
+        words = read_tile(got_refs, p * tiles + t)
         even.append((words << 16).astype(f32) * even_step)
         odd.append((words >> 16).astype(f32) * odd_step)
     return [jnp.concatenate(even, axis=1), jnp.concatenate(odd, axis=1)]
@@ -179,11 +189,12 @@
     return [tall[:, s * lanes : (s + 1) * lanes] for s in range(slots)]
 
 
-def score_kernel(got_ref, sums_hbm, best_ref, sums_ref, sem):
+def score_kernel(mine_ref, other_ref, sums_hbm, best_ref, sums_ref, sem, *, members):
+    got_refs = (mine_ref, other_ref)
     owners = lanes
     total = slots * owners
     owned, width = sums_ref.shape
-    notes = read_notes(got_ref)
+    notes = read_notes(got_refs)
     sub = iota((8 * slots, lanes), 0)
     field = iota((8 * slots, lanes), 1) - fields * (sub // 8)
     kind = sub % 8
@@ -204,7 +215,7 @@
     step = along_sublanes(notes, 3)
     exact = []
     for p in range(pairs):
-        exact = exact + read_rows(got_ref, p, step)
+        exact = exact + read_rows(got_refs, p, step)
     exact = jnp.concatenate(exact, axis=0)
     keys = exact.astype(bf16)
     rest = (exact - keys.astype(f32)).astype(bf16)
@@ -227,7 +238,7 @@
     other = jnp.concatenate([key] * (block // lanes), axis=1)
     bests = []
     for start in range(0, total, block):
-        if start == 1 * block:
+        if start == 0 * block:
             centre()
         stop = start + block
         scores = dot(keys, keys[start:stop], ((1,), (1,)))
@@ -238,7 +249,14 @@
     rows = jnp.full((lanes, owners), -1.0, f32)
     for s in range(slots):
         rows = jnp.where(sub == s, best[:, s * owners : (s + 1) * owners], rows)
-    best_ref[...] = rows.T
+    rows = rows.T
+    north = jnp.broadcast_to(lax.axis_index("shard") % 2, (members, lanes)) == 1
+    for x in range(half // members):
+        first = rows[x * members : (x + 1) * members]
+        second = rows[half + x * members : half + (x + 1) * members]
+        at = 2 * x * members
+        best_ref[at : at + members, :] = jnp.where(north, second, first)
+        best_ref[at + members : at + 2 * members, :] = jnp.where(north, first, second)
     copy.wait()
 
 
@@ -262,14 +280,16 @@
 
 
 def shards(embeddings, clusters, row_ids, owner_map):
-    owners = lax.axis_size("shard") * lax.axis_size("member")
+    shard_count = lax.axis_size("shard")
+    members = lax.axis_size("member")
+    owners = shard_count * members
     local_rows, width = embeddings.shape
     cluster_count = owner_map.shape[0]
     per_owner = cluster_count // owners
     tiles = pairs * (width // lanes) + 1
     hbm = pl.BlockSpec(memory_space=pltpu.HBM)
     packed, route = pl.pallas_call(
-        functools.partial(pack_kernel, members=lax.axis_size("member")),
+        functools.partial(pack_kernel, members=members),
         in_specs=[hbm] * 4,
         out_shape=(
             jax.ShapeDtypeStruct((owners * tiles, lanes), i32),
@@ -295,11 +315,24 @@
             )
         ]
     )
-    packed = packed.reshape(owners, tiles, 1, lanes)
-    received = lax.all_to_all(packed, exchange, split_axis=0, concat_axis=0, tiled=True)
+    packed = packed.reshape(half, 2 * tiles, 1, lanes)
+    groups = [
+        [s * members + m for s in range(parity, shard_count, 2) for m in range(members)]
+        for parity in range(2)
+    ]
+    received = lax.all_to_all(
+        packed, axes, split_axis=0, concat_axis=0, tiled=True, axis_index_groups=groups
+    )
     received = received.reshape(owners * tiles, lanes)
+    other = pl.pallas_call(
+        split_kernel,
+        out_shape=jax.ShapeDtypeStruct((half * tiles, lanes), i32),
+        compiler_params=params,
+        name="split",
+    )(received)
+    other = lax.ppermute(other, "shard", [(s, s ^ 1) for s in range(shard_count)])
     centroids, best = pl.pallas_call(
-        score_kernel,
+        functools.partial(score_kernel, members=members),
         out_shape=(
             jax.ShapeDtypeStruct((per_owner, width), f32),
             jax.ShapeDtypeStruct((owners, lanes), f32),
@@ -308,9 +341,9 @@
         scratch_shapes=[pltpu.VMEM((per_owner, width), f32), pltpu.SemaphoreType.DMA(())],
         compiler_params=params,
         name="score",
-    )(received)
+    )(received, other)
     returned = lax.all_to_all(
-        best.reshape(owners, 1, lanes), exchange, split_axis=0, concat_axis=0, tiled=True
+        best.reshape(owners, 1, lanes), axes, split_axis=0, concat_axis=0, tiled=True
     )
     earlier_max = pl.pallas_call(
         unpack_kernel,

time: 52.5 us -> 54.5 us (1.038)
  starting transfers between devices: 0 us -> 3.06 us
  blocking collectives: 46.4 us -> 43.8 us
  waiting for transfers between devices: 0 us -> 1.68 us
    ppermute x0 -> x1, starting transfers between devices: none -> 3.06 us  [shards(): lax.ppermute(other, 'shard', [(s, s ^ 1) for s in range(shard_count)])]
    all_to_all x2, blocking collectives: 46.4 us -> 43.8 us  [the longest x1 30.5 us: shards(): lax.all_to_all(packed, axes, split_axis=0, concat_axis=0, tiled=True, axi...]
    ppermute x0 -> x1, waiting for transfers between devices: none -> 1.68 us  [shards(): lax.ppermute(other, 'shard', [(s, s ^ 1) for s in range(shard_count)])]
    pallas_call x2 -> x3, Pallas kernels: 4.47 us -> 4.34 us  [the longest x1 2.25 us: shards(): pl.pallas_call(functools.partial(pack_kernel, members=members), in_specs=...]
  transfers between devices with their start and end apart: 0 -> 1, of which waited for: 0 -> 1; matrix products, arithmetic and copies ran while one was open for 0% -> 0% of each run, Pallas kernels for 0% -> 0%
where the time goes in v8:
time: 54.5 us; the launch traced here: 54.3 us
  blocking collectives  43.8 us (80%)
  Pallas kernels  5.12 us (9%)
  starting transfers between devices  3.06 us (6%)
  waiting for transfers between devices  1.68 us (3%)
  between operations  0.65 us (1%)
    all_to_all x1, blocking collectives, shards(): lax.all_to_all(packed, axes, split_axis=0, concat_axis=0, tiled=True, axi...  30.5 us
    all_to_all x1, blocking collectives, shards(): lax.all_to_all(best.reshape(owners, 1, lanes), axes, split_axis=0, concat...  13.3 us
    ppermute x1, starting transfers between devices, shards(): lax.ppermute(other, 'shard', [(s, s ^ 1) for s in range(shard_count)])  3.06 us
    pallas_call x1, Pallas kernels, shards(): pl.pallas_call(functools.partial(pack_kernel, members=members), in_specs=...  2.25 us
    pallas_call x1, Pallas kernels, shards(): pl.pallas_call(functools.partial(score_kernel, members=members), out_shap...  2.04 us
    ppermute x1, waiting for transfers between devices, shards(): lax.ppermute(other, 'shard', [(s, s ^ 1) for s in range(shard_count)])  1.68 us
  transfers between devices with their start and end apart: 1, of which 1 were waited for; matrix products, arithmetic and copies ran while one was open for 0% of the time, Pallas kernels for 0%

profile of v8, /device:TPU:1, one launch (start us, length us, event | category | flops | bytes accessed | tf_op | source)
XLA Modules:
  0.0 54.3 jit_solution(9712458059082344589)
XLA Ops:
  0.6 2.2 %pack.1 = (s32[2432,128]{1,0:T(8,128)S(1)}, s32[8,256]{1,0:T(8,128)S(1)}) custom-call(f32[256,768]{1,0:T(8,128)} %rows_hbm.1, s32[1,256]{1,0:T(1,128)} %bitcast.15, s32[1,256]{1,0:T(1,128)} %bitcast.16, s32[1,256]{1,0:T(1,128)} %bitcast.17), custom_call_target="tpu_custom_call" | custom-call | tf_op jit(solution)/shard_map/pack/pallas_call | solution.py:291
  2.9 30.5 %all_to_all.10 = s32[64,38,1,128]{3,2,1,0:T(1,128)S(1)} all-to-all(s32[64,38,1,128]{3,2,1,0:T(1,128)S(1)} %bitcast.12), channel_id=1, replica_groups={{0,1,2,3,4,5,6,7,8,9,10,11,12,13,14,15,32,33,34,35,36,37,38,39,40,41,42..., dimensions={0} | all-to-all | bytes 2490368 | tf_op jit(solution)/shard_map/all_to_all | solution.py:323
  33.4 0.1 split.1
  33.4 3.1 %collective-permute-start = (s32[1216,128]{1,0:T(8,128)S(1)}, s32[1216,128]{1,0:T(8,128)S(1)}, u32[]{:S(2)}, u32[]{:S(2)}) collective-permute-start(s32[1216,128]{1,0:T(8,128)S(1)} %split.1), channel_id=1, source_target_pairs={{0,16},{16,0},{32,48},{48,32},{64,80},{80,64},{96,112},{112,96},{1... | collective-permute-start | bytes 1867784 | tf_op jit(solution)/shard_map/ppermute | solution.py:333
  36.5 1.7 %collective-permute-done.other_ref = s32[1216,128]{1,0:T(8,128)S(1)} collective-permute-done((s32[1216,128]{1,0:T(8,128)S(1)}, s32[1216,128]{1,0:T(8,128)S(1)}, u32[]{:S(2)}, u32[]{:S(2)}) %collective-permute-start) | collective-permute-done | bytes 622624 | tf_op jit(solution)/shard_map/ppermute | solution.py:333
  38.2 2.0 %score.1 = (f32[2,768]{1,0:T(2,128)}, f32[128,128]{1,0:T(8,128)S(1)}) custom-call(s32[2432,128]{1,0:T(8,128)S(1)} %bitcast.11, s32[1216,128]{1,0:T(8,128)S(1)} %collective-permute-done.other_ref), custom_call_target="tpu_custom_call" | custom-call | tf_op jit(solution)/shard_map/score/pallas_call | solution.py:334
  40.2 13.3 %all_to_all.11 = f32[128,1,128]{2,1,0:T(1,128)S(1)} all-to-all(f32[128,1,128]{2,1,0:T(1,128)S(1)} %bitcast.14), channel_id=1, replica_groups=mesh['shard'=8,'member'=16] {'shard','member'}, dimensions={0} | all-to-all | bytes 131072 | tf_op jit(solution)/shard_map/all_to_all | solution.py:345
  53.5 0.8 %unpack.1 = f32[1,256]{1,0:T(1,128)} custom-call(f32[128,128]{1,0:T(8,128)S(1)} %bitcast.13, s32[8,256]{1,0:T(8,128)S(1)} %get-tuple-element.9.route_ref), custom_call_target="tpu_custom_call" | custom-call | tf_op jit(solution)/shard_map/unpack/pallas_call | solution.py:348
Async XLA Ops:
  33.4 4.7 %collective-permute-start = (s32[1216,128]{1,0:T(8,128)S(1)}, s32[1216,128]{1,0:T(8,128)S(1)}, u32[]{:S(2)}, u32[]{:S(2)}) collective-permute-start(s32[1216,128]{1,0:T(8,128)S(1)} %split.1), channel_id=1, source_target_pairs={{0,16},{16,0},{32,48},{48,32},{64,80},{80,64},{96,112},{112,96},{1... | collective-permute-start | bytes 1867784 | tf_op jit(solution)/shard_map/ppermute | solution.py:333

commit v9 on v7

--- a/solution.py
+++ b/solution.py
@@ -144,6 +144,8 @@
     words = dot(one_hot(mine), notes, ((1,), (1,))).astype(i32)
     sent_ref[pl.ds(tiles - 1, owners, tiles), :] = words
     sub = iota(route_ref.shape, 0)
+    shard_count = owners // members
+    owner = owner % shard_count * members + owner // shard_count
     route_ref[...] = jnp.where(sub == 0, owner, slot)
 
 
@@ -179,7 +181,7 @@
     return [tall[:, s * lanes : (s + 1) * lanes] for s in range(slots)]
 
 
-def score_kernel(got_ref, sums_hbm, best_ref, sums_ref, sem):
+def score_kernel(got_ref, sums_hbm, best_ref, sums_ref, sem, *, members):
     owners = lanes
     total = slots * owners
     owned, width = sums_ref.shape
@@ -227,7 +229,7 @@
     other = jnp.concatenate([key] * (block // lanes), axis=1)
     bests = []
     for start in range(0, total, block):
-        if start == 1 * block:
+        if start == 0 * block:
             centre()
         stop = start + block
         scores = dot(keys, keys[start:stop], ((1,), (1,)))
@@ -238,7 +240,10 @@
     rows = jnp.full((lanes, owners), -1.0, f32)
     for s in range(slots):
         rows = jnp.where(sub == s, best[:, s * owners : (s + 1) * owners], rows)
-    best_ref[...] = rows.T
+    rows = rows.T
+    shard_count = owners // members
+    for m in range(members):
+        best_ref[pl.ds(m, shard_count, members), :] = rows[m * shard_count : (m + 1) * shard_count]
     copy.wait()
 
 
@@ -299,7 +304,7 @@
     received = lax.all_to_all(packed, exchange, split_axis=0, concat_axis=0, tiled=True)
     received = received.reshape(owners * tiles, lanes)
     centroids, best = pl.pallas_call(
-        score_kernel,
+        functools.partial(score_kernel, members=lax.axis_size("member")),
         out_shape=(
             jax.ShapeDtypeStruct((per_owner, width), f32),
             jax.ShapeDtypeStruct((owners, lanes), f32),
@@ -310,7 +315,7 @@
         name="score",
     )(received)
     returned = lax.all_to_all(
-        best.reshape(owners, 1, lanes), exchange, split_axis=0, concat_axis=0, tiled=True
+        best.reshape(owners, 1, lanes), axes, split_axis=0, concat_axis=0, tiled=True
     )
     earlier_max = pl.pallas_call(
         unpack_kernel,

time: 52.5 us -> 52.5 us (level)
  no operation moved by 1% of the time
where the time goes in v9:
time: 52.5 us; the launch traced here: 52.3 us
  blocking collectives  46.6 us (89%)
  Pallas kernels  5.06 us (10%)
  between operations  0.65 us (1%)
    all_to_all x1, blocking collectives, shards(): lax.all_to_all(packed, exchange, split_axis=0, concat_axis=0, tiled=True)  32.6 us
    all_to_all x1, blocking collectives, shards(): lax.all_to_all(best.reshape(owners, 1, lanes), axes, split_axis=0, concat...  14 us
    pallas_call x1, Pallas kernels, shards(): pl.pallas_call(functools.partial(pack_kernel, members=lax.axis_size('memb...  2.24 us
    pallas_call x1, Pallas kernels, shards(): pl.pallas_call(functools.partial(score_kernel, members=lax.axis_size('mem...  2.04 us

profile of v9, /device:TPU:1, one launch (start us, length us, event | category | flops | bytes accessed | tf_op | source)
XLA Modules:
  0.0 52.3 jit_solution(8351521034980357632)
XLA Ops:
  0.6 2.2 %pack.1 = (s32[2432,128]{1,0:T(8,128)S(1)}, s32[8,256]{1,0:T(8,128)S(1)}) custom-call(f32[256,768]{1,0:T(8,128)} %rows_hbm.1, s32[1,256]{1,0:T(1,128)} %bitcast.14, s32[1,256]{1,0:T(1,128)} %bitcast.15, s32[1,256]{1,0:T(1,128)} %bitcast.16), custom_call_target="tpu_custom_call" | custom-call | tf_op jit(solution)/shard_map/pack/pallas_call | solution.py:276
  2.9 32.6 %all_to_all.10 = s32[128,19,1,128]{3,2,1,0:T(1,128)S(1)} all-to-all(s32[128,19,1,128]{3,2,1,0:T(1,128)S(1)} %bitcast.11), channel_id=1, replica_groups=mesh['shard'=8,'member'=16] {'member','shard'}, dimensions={0} | all-to-all | bytes 2490368 | tf_op jit(solution)/shard_map/all_to_all | solution.py:304
  35.5 2.0 %score.1 = (f32[2,768]{1,0:T(2,128)}, f32[128,128]{1,0:T(8,128)S(1)}) custom-call(s32[2432,128]{1,0:T(8,128)S(1)} %bitcast.10), custom_call_target="tpu_custom_call" | custom-call | tf_op jit(solution)/shard_map/score/pallas_call | solution.py:306
  37.6 14.0 %all_to_all.11 = f32[128,1,128]{2,1,0:T(1,128)S(1)} all-to-all(f32[128,1,128]{2,1,0:T(1,128)S(1)} %bitcast.13), channel_id=1, replica_groups=mesh['shard'=8,'member'=16] {'shard','member'}, dimensions={0} | all-to-all | bytes 131072 | tf_op jit(solution)/shard_map/all_to_all | solution.py:317
  51.5 0.8 %unpack.1 = f32[1,256]{1,0:T(1,128)} custom-call(f32[128,128]{1,0:T(8,128)S(1)} %bitcast.12, s32[8,256]{1,0:T(8,128)S(1)} %get-tuple-element.9.route_ref), custom_call_target="tpu_custom_call" | custom-call | tf_op jit(solution)/shard_map/unpack/pallas_call | solution.py:320

commit v10 on v7

--- a/solution.py
+++ b/solution.py
@@ -1,5 +1,3 @@
-import functools
-
 import jax
 import jax.numpy as jnp
 from jax import lax
@@ -9,7 +7,6 @@
 
 epsilon = 1e-06
 axes = ("shard", "member")
-exchange = ("member", "shard")
 pairs = 3
 slots = 2 * pairs
 lanes = 128
@@ -64,8 +61,6 @@
     ids_ref,
     owners_ref,
     sems,
-    *,
-    members,
 ):
     index_copies = (
         pltpu.make_async_copy(owners_hbm, owners_ref, sems.at[0]),
@@ -80,9 +75,7 @@
         index_copy.wait()
     clusters = clusters_ref[...]
     ids = ids_ref[...]
-    owner_map = owners_ref[...]
-    owner_map = owner_map % members * (lanes // members) + owner_map // members
-    owner_map = owner_map.astype(f32)
+    owner_map = owners_ref[...].astype(f32)
     row_count, width = rows_ref.shape
     tiles = pairs * (width // lanes) + 1
     owners = sent_ref.shape[0] // tiles
@@ -179,7 +172,7 @@
     return [tall[:, s * lanes : (s + 1) * lanes] for s in range(slots)]
 
 
-def score_kernel(got_ref, sums_hbm, best_ref, sums_ref, sem):
+def score_kernel(got_ref, sums_ref, best_ref):
     owners = lanes
     total = slots * owners
     owned, width = sums_ref.shape
@@ -209,8 +202,6 @@
     keys = exact.astype(bf16)
     rest = (exact - keys.astype(f32)).astype(bf16)
 
-    copy = pltpu.make_async_copy(sums_ref, sums_hbm, sem)
-
     def centre():
         sub = iota((8, total), 0)
         coarse = line[2].astype(bf16).astype(f32)
@@ -221,7 +212,6 @@
         sums = sums[0:owned] + sums[owned : 2 * owned]
         scale = lax.rsqrt(jnp.mean(sums * sums, axis=1, keepdims=True) + epsilon)
         sums_ref[...] = sums * scale
-        copy.start()
 
     block = 2 * lanes
     other = jnp.concatenate([key] * (block // lanes), axis=1)
@@ -239,7 +229,6 @@
     for s in range(slots):
         rows = jnp.where(sub == s, best[:, s * owners : (s + 1) * owners], rows)
     best_ref[...] = rows.T
-    copy.wait()
 
 
 def exact_dot(values, hot, contract=((1,), (0,))):
@@ -250,7 +239,8 @@
     return dot(first, hot, contract) + dot(second, hot, contract) + dot(third, hot, contract)
 
 
-def unpack_kernel(back_ref, route_ref, out_ref):
+def unpack_kernel(back_ref, route_ref, sums_ref, centres_ref, out_ref):
+    centres_ref[...] = sums_ref[...]
     owner = route_ref[0:1, :]
     slot = route_ref[1:2, :]
     back = back_ref[...]
@@ -269,7 +259,7 @@
     tiles = pairs * (width // lanes) + 1
     hbm = pl.BlockSpec(memory_space=pltpu.HBM)
     packed, route = pl.pallas_call(
-        functools.partial(pack_kernel, members=lax.axis_size("member")),
+        pack_kernel,
         in_specs=[hbm] * 4,
         out_shape=(
             jax.ShapeDtypeStruct((owners * tiles, lanes), i32),
@@ -296,7 +286,7 @@
         ]
     )
     packed = packed.reshape(owners, tiles, 1, lanes)
-    received = lax.all_to_all(packed, exchange, split_axis=0, concat_axis=0, tiled=True)
+    received = lax.all_to_all(packed, axes, split_axis=0, concat_axis=0, tiled=True)
     received = received.reshape(owners * tiles, lanes)
     centroids, best = pl.pallas_call(
         score_kernel,
@@ -304,20 +294,21 @@
             jax.ShapeDtypeStruct((per_owner, width), f32),
             jax.ShapeDtypeStruct((owners, lanes), f32),
         ),
-        out_specs=(hbm, pl.BlockSpec(memory_space=pltpu.VMEM)),
-        scratch_shapes=[pltpu.VMEM((per_owner, width), f32), pltpu.SemaphoreType.DMA(())],
         compiler_params=params,
         name="score",
     )(received)
     returned = lax.all_to_all(
-        best.reshape(owners, 1, lanes), exchange, split_axis=0, concat_axis=0, tiled=True
+        best.reshape(owners, 1, lanes), axes, split_axis=0, concat_axis=0, tiled=True
     )
-    earlier_max = pl.pallas_call(
+    centroids, earlier_max = pl.pallas_call(
         unpack_kernel,
-        out_shape=jax.ShapeDtypeStruct((1, local_rows), f32),
+        out_shape=(
+            jax.ShapeDtypeStruct((per_owner, width), f32),
+            jax.ShapeDtypeStruct((1, local_rows), f32),
+        ),
         compiler_params=params,
         name="unpack",
-    )(returned.reshape(owners, lanes), route)
+    )(returned.reshape(owners, lanes), route, centroids)
     return (centroids, earlier_max.reshape(local_rows))
 
 

time: 52.5 us -> 51.9 us (0.989)
  no operation moved by 1% of the time
where the time goes in v10:
time: 51.9 us; the launch traced here: 51.7 us
  blocking collectives  46.1 us (89%)
  Pallas kernels  4.92 us (9%)
  between operations  0.65 us (1%)
    all_to_all x1, blocking collectives, shards(): lax.all_to_all(packed, axes, split_axis=0, concat_axis=0, tiled=True)  32.1 us
    all_to_all x1, blocking collectives, shards(): lax.all_to_all(best.reshape(owners, 1, lanes), axes, split_axis=0, concat...  14.1 us
    pallas_call x1, Pallas kernels, shards(): pl.pallas_call(pack_kernel, in_specs=[hbm] * 4, out_shape=(jax.ShapeDtype...  2.23 us
    pallas_call x1, Pallas kernels, shards(): pl.pallas_call(score_kernel, out_shape=(jax.ShapeDtypeStruct((per_owner,...  1.91 us

profile of v10, /device:TPU:1, one launch (start us, length us, event | category | flops | bytes accessed | tf_op | source)
XLA Modules:
  0.0 51.7 jit_solution(16474799647268736363)
XLA Ops:
  0.6 2.2 %pack.1 = (s32[2432,128]{1,0:T(8,128)S(1)}, s32[8,256]{1,0:T(8,128)S(1)}) custom-call(f32[256,768]{1,0:T(8,128)} %rows_hbm.1, s32[1,256]{1,0:T(1,128)} %bitcast.14, s32[1,256]{1,0:T(1,128)} %bitcast.15, s32[1,256]{1,0:T(1,128)} %bitcast.16), custom_call_target="tpu_custom_call" | custom-call | tf_op jit(solution)/shard_map/pack/pallas_call | solution.py:261
  2.9 32.1 %all_to_all.10 = s32[128,19,1,128]{3,2,1,0:T(1,128)S(1)} all-to-all(s32[128,19,1,128]{3,2,1,0:T(1,128)S(1)} %bitcast.11), channel_id=1, replica_groups=mesh['shard'=8,'member'=16] {'shard','member'}, dimensions={0} | all-to-all | bytes 2490368 | tf_op jit(solution)/shard_map/all_to_all | solution.py:289
  34.9 1.9 %score.1 = (f32[2,768]{1,0:T(2,128)S(1)}, f32[128,128]{1,0:T(8,128)S(1)}) custom-call(s32[2432,128]{1,0:T(8,128)S(1)} %bitcast.10), custom_call_target="tpu_custom_call" | custom-call | tf_op jit(solution)/shard_map/score/pallas_call | solution.py:291
  36.9 14.1 %all_to_all.11 = f32[128,1,128]{2,1,0:T(1,128)S(1)} all-to-all(f32[128,1,128]{2,1,0:T(1,128)S(1)} %bitcast.13), channel_id=1, replica_groups=mesh['shard'=8,'member'=16] {'shard','member'}, dimensions={0} | all-to-all | bytes 131072 | tf_op jit(solution)/shard_map/all_to_all | solution.py:300
  50.9 0.8 %unpack.1 = (f32[2,768]{1,0:T(2,128)}, f32[1,256]{1,0:T(1,128)}) custom-call(f32[128,128]{1,0:T(8,128)S(1)} %bitcast.12, s32[8,256]{1,0:T(8,128)S(1)} %get-tuple-element.10.route_ref, f32[2,768]{1,0:T(2,128)S(1)} %get-tuple-element.11.sums_ref), custom_call_target="tpu_custom_call" | custom-call | tf_op jit(solution)/shard_map/unpack/pallas_call | solution.py:303

commit v11 on v10

--- a/solution.py
+++ b/solution.py
@@ -104,6 +104,12 @@
     largest = jnp.max(jnp.abs(rows), axis=1, keepdims=True) * inverse
     step = jnp.clip(jnp.ceil(largest * full), 1.0, full)
     codes = jnp.floor(rows * (inverse * (full * full / step)) + 0.5)
+    wanted = (rows * inverse).astype(bf16).astype(f32)
+    reached = (codes * (step * (1.0 / (full * full)))).astype(bf16).astype(f32)
+    missing = wanted - reached
+    least = step * (0.9 / (full * full))
+    codes = codes + jnp.where(missing >= least, 1.0, jnp.where(missing <= -least, -1.0, 0.0))
+    codes = jnp.clip(codes, -full, full)
     upper = codes.astype(bf16)
     halves = jnp.concatenate([upper, (codes - upper.astype(f32)).astype(bf16)], axis=0)
     norm_row = jnp.sum(jnp.where(diagonal, norm, 0.0), axis=0, keepdims=True)

time: 51.9 us -> 52.2 us (level)
  no operation moved by 1% of the time
where the time goes in v11:
time: 52.2 us; the launch traced here: 52.1 us
  blocking collectives  46.1 us (88%)
  Pallas kernels  5.29 us (10%)
  between operations  0.65 us (1%)
    all_to_all x1, blocking collectives, shards(): lax.all_to_all(packed, axes, split_axis=0, concat_axis=0, tiled=True)  32.1 us
    all_to_all x1, blocking collectives, shards(): lax.all_to_all(best.reshape(owners, 1, lanes), axes, split_axis=0, concat...  14.1 us
    pallas_call x1, Pallas kernels, shards(): pl.pallas_call(pack_kernel, in_specs=[hbm] * 4, out_shape=(jax.ShapeDtype...  2.61 us
    pallas_call x1, Pallas kernels, shards(): pl.pallas_call(score_kernel, out_shape=(jax.ShapeDtypeStruct((per_owner,...  1.91 us

profile of v11, /device:TPU:1, one launch (start us, length us, event | category | flops | bytes accessed | tf_op | source)
XLA Modules:
  0.0 52.1 jit_solution(8384114168169348951)
XLA Ops:
  0.6 2.6 %pack.1 = (s32[2432,128]{1,0:T(8,128)S(1)}, s32[8,256]{1,0:T(8,128)S(1)}) custom-call(f32[256,768]{1,0:T(8,128)} %rows_hbm.1, s32[1,256]{1,0:T(1,128)} %bitcast.14, s32[1,256]{1,0:T(1,128)} %bitcast.15, s32[1,256]{1,0:T(1,128)} %bitcast.16), custom_call_target="tpu_custom_call" | custom-call | tf_op jit(solution)/shard_map/pack/pallas_call | solution.py:267
  3.2 32.1 %all_to_all.10 = s32[128,19,1,128]{3,2,1,0:T(1,128)S(1)} all-to-all(s32[128,19,1,128]{3,2,1,0:T(1,128)S(1)} %bitcast.11), channel_id=1, replica_groups=mesh['shard'=8,'member'=16] {'shard','member'}, dimensions={0} | all-to-all | bytes 2490368 | tf_op jit(solution)/shard_map/all_to_all | solution.py:295
  35.3 1.9 %score.1 = (f32[2,768]{1,0:T(2,128)S(1)}, f32[128,128]{1,0:T(8,128)S(1)}) custom-call(s32[2432,128]{1,0:T(8,128)S(1)} %bitcast.10), custom_call_target="tpu_custom_call" | custom-call | tf_op jit(solution)/shard_map/score/pallas_call | solution.py:297
  37.2 14.1 %all_to_all.11 = f32[128,1,128]{2,1,0:T(1,128)S(1)} all-to-all(f32[128,1,128]{2,1,0:T(1,128)S(1)} %bitcast.13), channel_id=1, replica_groups=mesh['shard'=8,'member'=16] {'shard','member'}, dimensions={0} | all-to-all | bytes 131072 | tf_op jit(solution)/shard_map/all_to_all | solution.py:306
  51.3 0.8 %unpack.1 = (f32[2,768]{1,0:T(2,128)}, f32[1,256]{1,0:T(1,128)}) custom-call(f32[128,128]{1,0:T(8,128)S(1)} %bitcast.12, s32[8,256]{1,0:T(8,128)S(1)} %get-tuple-element.10.route_ref, f32[2,768]{1,0:T(2,128)S(1)} %get-tuple-element.11.sums_ref), custom_call_target="tpu_custom_call" | custom-call | tf_op jit(solution)/shard_map/unpack/pallas_call | solution.py:309

commit v12 on v10

--- a/solution.py
+++ b/solution.py
@@ -73,6 +73,7 @@
     copy.start()
     for index_copy in index_copies:
         index_copy.wait()
+    copy.wait()
     clusters = clusters_ref[...]
     ids = ids_ref[...]
     owner_map = owners_ref[...].astype(f32)
@@ -96,7 +97,6 @@
     owner = found[0:1].astype(i32)
     rank = found[1:2].astype(i32)
 
-    copy.wait()
     rows = rows_ref[...]
     power = jnp.sum(rows * rows, axis=1, keepdims=True) + epsilon
     inverse = lax.rsqrt(power)

time: 51.9 us -> 52.1 us (level)
  no operation moved by 1% of the time
where the time goes in v12:
time: 52.1 us; the launch traced here: 52 us
  blocking collectives  46.1 us (88%)
  Pallas kernels  5.19 us (10%)
  between operations  0.65 us (1%)
    all_to_all x1, blocking collectives, shards(): lax.all_to_all(packed, axes, split_axis=0, concat_axis=0, tiled=True)  32.1 us
    all_to_all x1, blocking collectives, shards(): lax.all_to_all(best.reshape(owners, 1, lanes), axes, split_axis=0, concat...  14.1 us
    pallas_call x1, Pallas kernels, shards(): pl.pallas_call(pack_kernel, in_specs=[hbm] * 4, out_shape=(jax.ShapeDtype...  2.51 us
    pallas_call x1, Pallas kernels, shards(): pl.pallas_call(score_kernel, out_shape=(jax.ShapeDtypeStruct((per_owner,...  1.91 us

profile of v12, /device:TPU:1, one launch (start us, length us, event | category | flops | bytes accessed | tf_op | source)
XLA Modules:
  0.0 52.0 jit_solution(428007540992720739)
XLA Ops:
  0.6 2.5 %pack.1 = (s32[2432,128]{1,0:T(8,128)S(1)}, s32[8,256]{1,0:T(8,128)S(1)}) custom-call(f32[256,768]{1,0:T(8,128)} %rows_hbm.1, s32[1,256]{1,0:T(1,128)} %bitcast.14, s32[1,256]{1,0:T(1,128)} %bitcast.15, s32[1,256]{1,0:T(1,128)} %bitcast.16), custom_call_target="tpu_custom_call" | custom-call | tf_op jit(solution)/shard_map/pack/pallas_call | solution.py:261
  3.1 32.1 %all_to_all.10 = s32[128,19,1,128]{3,2,1,0:T(1,128)S(1)} all-to-all(s32[128,19,1,128]{3,2,1,0:T(1,128)S(1)} %bitcast.11), channel_id=1, replica_groups=mesh['shard'=8,'member'=16] {'shard','member'}, dimensions={0} | all-to-all | bytes 2490368 | tf_op jit(solution)/shard_map/all_to_all | solution.py:289
  35.2 1.9 %score.1 = (f32[2,768]{1,0:T(2,128)S(1)}, f32[128,128]{1,0:T(8,128)S(1)}) custom-call(s32[2432,128]{1,0:T(8,128)S(1)} %bitcast.10), custom_call_target="tpu_custom_call" | custom-call | tf_op jit(solution)/shard_map/score/pallas_call | solution.py:291
  37.1 14.1 %all_to_all.11 = f32[128,1,128]{2,1,0:T(1,128)S(1)} all-to-all(f32[128,1,128]{2,1,0:T(1,128)S(1)} %bitcast.13), channel_id=1, replica_groups=mesh['shard'=8,'member'=16] {'shard','member'}, dimensions={0} | all-to-all | bytes 131072 | tf_op jit(solution)/shard_map/all_to_all | solution.py:300
  51.2 0.8 %unpack.1 = (f32[2,768]{1,0:T(2,128)}, f32[1,256]{1,0:T(1,128)}) custom-call(f32[128,128]{1,0:T(8,128)S(1)} %bitcast.12, s32[8,256]{1,0:T(8,128)S(1)} %get-tuple-element.10.route_ref, f32[2,768]{1,0:T(2,128)S(1)} %get-tuple-element.11.sums_ref), custom_call_target="tpu_custom_call" | custom-call | tf_op jit(solution)/shard_map/unpack/pallas_call | solution.py:303
